TPU v7x, 128 devices: a whole 4x4x4 slice. The times are simulated.
128 devices in a mesh: rep: 2 (over core), dp: 64 (over x, y, z).
Axes of the slice: x: 4, y: 4, z: 4, core: 2. Of those that a mesh axis runs over, the one named last changes fastest.
Arguments:
- x: bfloat16 [128, 2048, 1024], P(('rep', 'dp')), parts along dimension 0
- dy: bfloat16 [128, 2048, 1024], P(('rep', 'dp')), parts along dimension 0
- w_gate: bfloat16 [2, 1024, 2816], replicated
- w_up: bfloat16 [2, 1024, 2816], replicated
- w_down: bfloat16 [2, 2816, 1024], replicated
- m_w_gate: float32 [2, 1024, 2816], P(None, 'dp')
- m_w_up: float32 [2, 1024, 2816], P(None, 'dp')
- m_w_down: float32 [2, 2816, 1024], P(None, 'dp')
- v_w_gate: float32 [2, 1024, 2816], P(None, 'dp')
- v_w_up: float32 [2, 1024, 2816], P(None, 'dp')
- v_w_down: float32 [2, 2816, 1024], P(None, 'dp')
Outputs:
- output 1: bfloat16 [4, 1024, 2816], P('rep'), parts along dimension 0
- output 2: bfloat16 [4, 1024, 2816], P('rep'), parts along dimension 0
- output 3: bfloat16 [4, 2816, 1024], P('rep'), parts along dimension 0
- output 4: float32 [4, 1024, 2816], P('rep', 'dp'), parts along dimension 0
- output 5: float32 [4, 1024, 2816], P('rep', 'dp'), parts along dimension 0
- output 6: float32 [4, 2816, 1024], P('rep', 'dp'), parts along dimension 0
- output 7: float32 [4, 1024, 2816], P('rep', 'dp'), parts along dimension 0
- output 8: float32 [4, 1024, 2816], P('rep', 'dp'), parts along dimension 0
- output 9: float32 [4, 2816, 1024], P('rep', 'dp'), parts along dimension 0
There are 2 independent parts. A program takes and returns all parts, laid end to end along the dimension named above; an argument that names none is the same for every part.
All inputs are finite; a program needn't handle non-finite values.
Results may differ from a plain program's by a relative error of at most 0.022.
Values are sent between devices in bfloat16 or wider.
A program may use at most 1.5 GiB of HBM per device.

v0:
```python
import jax
import jax.numpy as jnp
from jax import lax

NAMES = ("w_gate", "w_up", "w_down")


def matmul(a, w):
    return jnp.dot(a, w, preferred_element_type=jnp.float32).astype(jnp.bfloat16)


def normed(h):
    wide = h.astype(jnp.float32)
    scale = lax.rsqrt(jnp.mean(wide**2, -1, keepdims=True) + 1e-6)
    return (wide * scale).astype(jnp.bfloat16)


def layer(h, w):
    a = normed(h)
    gate = jnp.dot(a, w["w_gate"], preferred_element_type=jnp.float32)
    up = jnp.dot(a, w["w_up"], preferred_element_type=jnp.float32)
    return h + matmul((jax.nn.silu(gate) * up).astype(jnp.bfloat16), w["w_down"])


def adamw(w, m, v, g):
    m = 0.9 * m + 0.1 * g
    v = 0.95 * v + 0.05 * g * g
    step = m * lax.rsqrt(v + 1e-8) + 0.1 * w
    return (w - 0.02 * step).astype(jnp.bfloat16), m, v


def clipped(gradients, sum_of_squares, count):
    factor = jnp.minimum(1.0, 0.5 * lax.rsqrt(sum_of_squares / count + 1e-30))
    return [g * factor for g in gradients]


def stack(weights, h):
    for number in range(weights["w_gate"].shape[0]):
        h = layer(h, {name: w[number] for name, w in weights.items()})
    return h


def solution(mesh):
    groups = mesh.shape["rep"]

    def step(x, dy, *arrays):
        weights, m, v = (arrays[i : i + 3] for i in (0, 3, 6))
        x, dy = (t.reshape(groups, -1, *t.shape[1:]) for t in (x, dy))

        def of_a_group(x, dy):
            _, back = jax.vjp(lambda w: stack(w, x), dict(zip(NAMES, weights, strict=True)))
            by_weights = back(dy)[0]
            gradients = [by_weights[name].astype(jnp.float32) for name in NAMES]
            gradients = clipped(gradients, sum(jnp.sum(g * g) for g in gradients), sum(g.size for g in gradients))
            new = [adamw(w.astype(jnp.float32), m, v, g) for w, m, v, g in zip(weights, m, v, gradients, strict=True)]
            return tuple(one[which] for which in range(3) for one in new)

        return tuple(t.reshape(-1, *t.shape[2:]) for t in jax.vmap(of_a_group)(x, dy))

    return step
```

profile of v0, /device:TPU:0, one launch (start us, length us, event | category | flops | bytes accessed | tf_op | source)
XLA Modules:
  0.0 2175.4 jit_solution(899521243283835859)
XLA Ops:
  7.2 3.1 fusion.37
  10.3 6.5 copy.6
  16.8 19.9 fusion.69
  36.8 18.4 fusion.67
  55.1 17.0 convolution_convert_fusion.1
  72.2 19.6 fusion.28
  91.8 19.6 fusion.41
  111.3 0.6 copy-done.11
  112.0 20.2 fusion.58
  132.2 23.9 %fusion.44 = f32[1,1024,2816]{2,1,0:T(8,128)} fusion(bf16[2048,2816]{1,0:T(8,128)(2,1)} %convolution_convert_fusion.1, f32[2048,2816]{1,0:T(8,128)} %fusion.58, bf16[1,1,2048,1024]{2,3,1,0:T(8,128)(2,1)} %get-tuple-element.44, f32[2048]{0:T(1024)S(1)} %bitcast.364), kind=kOutput, calls=%fused_computation.60 | convolution fusion | flops 11852054528 | bytes 50339840 | tf_op jit(solution)/vmap(transpose(jvp()))/dot_general | solution.py:21
  156.2 6.8 copy.7
  163.0 20.1 fusion.61
  183.1 20.9 fusion.8
  204.0 20.6 fusion.26
  224.6 20.2 fusion.43
  244.8 5.3 fusion.83
  250.2 2.0 copy-done.3
  252.2 17.5 convolution_convert_fusion
  269.7 23.3 %fusion.47 = f32[1,1024,2816]{2,1,0:T(8,128)} fusion(bf16[2048,2816]{1,0:T(8,128)(2,1)} %convolution_convert_fusion, f32[2048,2816]{1,0:T(8,128)} %fusion.69, bf16[1,2048,1024]{1,2,0:T(8,128)(2,1)} %copy.6, f32[2048]{0:T(1024)S(1)} %copy-done.14), kind=kOutput, calls=%fused_computation.61 | convolution fusion | flops 11852054528 | bytes 50339840 | tf_op jit(solution)/vmap(transpose(jvp()))/dot_general | solution.py:21
  293.0 0.0 reduce-scatter.21.cloned.1.call-start
  293.0 19.2 convolution_bitcast_fusion.1
  312.3 28.4 %fusion.53 = f32[1,1024,2816]{2,1,0:T(8,128)} fusion(f32[2048,2816]{1,0:T(8,128)} %fusion.69, f32[2048,2816]{1,0:T(8,128)} %fusion.67, bf16[2048,2816]{1,0:T(8,128)(2,1)} %convolution_convert_fusion, bf16[1,2048,1024]{1,2,0:T(8,128)(2,1)} %copy.6, f32[2048]{0:T(1024)S(1)} %copy-done.14), kind=kOutput, calls=%fused_computation.65 | convolution fusion | flops 11880890368 | bytes 73408512 | tf_op jit(solution)/vmap(transpose(jvp()))/dot_general | solution.py:20
  340.8 19.2 convolution_bitcast_fusion
  359.9 24.3 %fusion.50 = f32[1,2816,1024]{2,1,0:T(8,128)} fusion(f32[2048,2816]{1,0:T(8,128)} %fusion.61, f32[2048,2816]{1,0:T(8,128)} %fusion.58, bf16[1,2048,1024]{2,1,0:T(8,128)(2,1)S(1)} %copy-done.5), kind=kOutput, calls=%fused_computation.62 | convolution fusion | flops 11845763072 | bytes 61865984 | tf_op jit(solution)/vmap(transpose(jvp()))/dot_general | solution.py:9
  384.3 454.9 %fusion.139 = (f32[48,1024]{1,0:T(8,128)S(1)}, f32[48,1024]{1,0:T(8,128)S(1)}) fusion(f32[1,2816,1024]{2,1,0:T(8,128)} %convolution_bitcast_fusion, f32[1,2816,1024]{2,1,0:T(8,128)} %fusion.50), kind=kCustom, calls=%all-reduce-scatter.2 | all-reduce-scatter fusion | flops 6291457 | bytes 23462400
  839.2 1.3 collective-permute-start.5
  840.6 1.3 collective-permute-start.11
  841.9 1.3 collective-permute-start.1
  843.2 2.8 collective-permute-start.2
  846.0 4.8 collective-permute-start.3
  850.8 3.4 collective-permute-start.4
  854.2 1.8 collective-permute-start
  856.0 5.3 collective-permute-start.7
  861.3 1.9 collective-permute-start.8
  863.2 1.3 collective-permute-start.9
  864.5 1.9 collective-permute-start.10
  866.5 2.6 collective-permute-start.6
  869.1 0.6 fusion.142
  871.0 1.4 concatenate
  872.4 0.6 copy-done.10
  873.1 2.7 concatenate.1
  875.9 0.7 fusion.103
  876.6 0.9 convert_bitcast_fusion.4
  877.5 73.2 %reduce-scatter.27.cloned.1.call-done = f32[1,16,2816]{2,1,0:T(8,128)} async-done(((f32[1,1024,2816]{2,1,0:T(8,128)}), f32[1,16,2816]{2,1,0:T(8,128)}) %reduce-scatter.27.cloned.1.call-update) | async-done | bytes 180240
  950.7 0.9 convert_bitcast_fusion.3
  951.6 0.7 fusion.118
  952.3 373.1 %reduce-scatter.21.cloned.1.call-done = f32[1,16,2816]{2,1,0:T(8,128)} async-done(((f32[1,1024,2816]{2,1,0:T(8,128)}), f32[1,16,2816]{2,1,0:T(8,128)}) %reduce-scatter.21.cloned.1.call-update) | async-done | bytes 180240
  1325.4 0.9 convert_bitcast_fusion.6
  1326.3 374.4 %reduce-scatter.23.cloned.1.call-done = f32[1,16,2816]{2,1,0:T(8,128)} async-done(((f32[1,1024,2816]{2,1,0:T(8,128)}), f32[1,16,2816]{2,1,0:T(8,128)}) %reduce-scatter.23.cloned.1.call-update) | async-done | bytes 180240
  1700.8 0.9 convert_bitcast_fusion.5
  1701.7 0.7 fusion.117
  1704.3 173.2 %all-reduce.10 = f32[1]{0:T(128)} all-reduce(f32[1]{0:T(128)} %bitcast.50), channel_id=3, replica_groups=mesh['rep'=2,'dp'=64] {'dp'}, use_global_device_ids=true, to_apply=%region_3.4.clone | all-reduce | flops 1 | bytes 8 | tf_op jit(solution)/vmap()/reduce_sum | solution.py:54
  1878.2 2.0 fusion.129
  1880.4 2.0 fusion.130
  1882.5 1.6 fusion.131
  1884.1 0.9 copy.10
  1885.0 1.0 copy.13
  1886.0 1.0 copy.12
  1887.0 76.6 %all-gather.12.cloned.1.call-done = bf16[1,2,1024,2816]{3,2,1,0:T(8,128)(2,1)} async-done(((bf16[1,2,16,2816]{3,2,1,0:T(8,128)(2,1)}), bf16[1,2,1024,2816]{3,2,1,0:T(8,128)(2,1)}) %all-gather.12.cloned.1.call-update) | async-done | bytes 11534352 | tf_op jit(solution)/reshape | solution.py:58
  1963.6 91.1 %all-gather.10.cloned.1.call-done = bf16[1,2,1024,2816]{3,2,1,0:T(8,128)(2,1)} async-done(((bf16[1,2,16,2816]{3,2,1,0:T(8,128)(2,1)}), bf16[1,2,1024,2816]{3,2,1,0:T(8,128)(2,1)}) %all-gather.10.cloned.1.call-update) | async-done | bytes 11534352 | tf_op jit(solution)/reshape | solution.py:58
  2054.7 90.8 %all-gather.14.cloned.1.call-done = bf16[1,2,2816,1024]{3,1,0,2:T(2,128)(2,1)} async-done(((bf16[1,2,44,1024]{3,1,0,2:T(2,128)(2,1)}), bf16[1,2,2816,1024]{3,1,0,2:T(2,128)(2,1)}) %all-gather.14.cloned.1.call-update) | async-done | bytes 11534352 | tf_op jit(solution)/reshape | solution.py:58
  2145.5 13.5 copy.11
  2159.0 4.9 copy.34
  2163.9 4.4 copy.35
  (79 shorter events, 0.7 us)
Async XLA Ops:
  7.2 869.4 %reduce-scatter.25.cloned.1.call-start = ((), (), s32[]{:S(2)}) async-start(), calls=%async_computation.9 | async-start | bytes 11714560
  16.8 20.0 copy-start.13
  16.8 20.0 copy-start.1
  36.8 18.4 copy-start.4
  111.3 0.6 copy-start.11
  156.1 794.6 %reduce-scatter.27.cloned.1.call-start = ((), (), s32[]{:S(2)}) async-start(), calls=%async_computation.10 | async-start | bytes 11714560
  156.1 27.0 %slice-start.3 = ((s8[11534336]{0:T(1024)(128)(4,1)}), s8[3145728]{0:T(1024)(128)(4,1)S(1)}, s32[]{:S(2)}) async-start(s8[11534336]{0:T(1024)(128)(4,1)} %bitcast.358), calls=%async_computation.14 | async-start | bytes 6291456
  163.0 20.1 slice-start.4
  163.0 20.1 slice-start.5
  224.6 20.2 copy-start.12
  224.6 20.2 copy-start
  250.2 2.0 copy-start.3
  252.2 17.5 copy-start.14
  293.0 1032.4 %reduce-scatter.21.cloned.1.call-start = ((), (), s32[]{:S(2)}) async-start(), calls=%async_computation.7 | async-start | bytes 11714560
  312.2 1388.5 %reduce-scatter.23.cloned.1.call-start = ((), (), s32[]{:S(2)}) async-start(), calls=%async_computation.8 | async-start | bytes 11714560
  340.7 1622.9 %all-gather.12.cloned.1.call-start = ((), (), s32[]{:S(2)}) async-start(), calls=%async_computation.5 | async-start | bytes 11714560 | tf_op jit(solution)/reshape | solution.py:58
  340.8 19.2 copy-start.5
  384.3 484.8 %copy-start.15 = (u32[128]{0:T(128)S(1)}, u32[128]{0:T(128)}, u32[]{:S(2)}) copy-start(u32[128]{0:T(128)} %constant.74) | copy-start | bytes 1540
  384.3 1493.9 %copy-start.6 = (f32[2,16,2816]{2,1,0:T(8,128)S(1)}, f32[2,16,2816]{2,1,0:T(8,128)}, u32[]{:S(2)}) copy-start(f32[2,16,2816]{2,1,0:T(8,128)} %param.8) | copy-start | bytes 1081348
  384.3 1494.0 %copy-start.7 = (f32[2,16,2816]{2,1,0:T(8,128)S(1)}, f32[2,16,2816]{2,1,0:T(8,128)}, u32[]{:S(2)}) copy-start(f32[2,16,2816]{2,1,0:T(8,128)} %param.7) | copy-start | bytes 1081348
  384.3 1496.1 %copy-start.8 = (f32[2,16,2816]{2,1,0:T(8,128)S(1)}, f32[2,16,2816]{2,1,0:T(8,128)}, u32[]{:S(2)}) copy-start(f32[2,16,2816]{2,1,0:T(8,128)} %param.6) | copy-start | bytes 1081348
  384.3 1496.1 %copy-start.9 = (f32[2,16,2816]{2,1,0:T(8,128)S(1)}, f32[2,16,2816]{2,1,0:T(8,128)}, u32[]{:S(2)}) copy-start(f32[2,16,2816]{2,1,0:T(8,128)} %param.1) | copy-start | bytes 1081348
  839.2 11.5 collective-permute-start.5
  840.6 13.6 collective-permute-start.11
  841.9 14.2 collective-permute-start.1
  843.2 18.1 collective-permute-start.2
  846.0 17.2 collective-permute-start.3
  850.8 13.7 collective-permute-start.4
  854.2 12.3 collective-permute-start
  856.0 16.3 collective-permute-start.7
  861.3 11.1 collective-permute-start.8
  863.2 9.2 collective-permute-start.9
  864.5 7.9 collective-permute-start.10
  866.5 6.6 collective-permute-start.6
  872.4 0.6 copy-start.10
  1880.3 174.4 %all-gather.10.cloned.1.call-start = ((), (), s32[]{:S(2)}) async-start(), calls=%async_computation.4 | async-start | bytes 11714560 | tf_op jit(solution)/reshape | solution.py:58
  1882.4 263.0 %all-gather.14.cloned.1.call-start = ((), (), s32[]{:S(2)}) async-start(), calls=%async_computation.6 | async-start | bytes 11714560 | tf_op jit(solution)/reshape | solution.py:58
  2145.5 13.5 copy-start.2
  2145.5 18.4 slice-start
  2145.5 18.4 slice-start.1
  2159.0 4.9 slice-start.2
Sparse Core Ops, SparseCore 0:
  156.2 394.7 reduce-scatter.24
  553.4 397.2 reduce-scatter.26
  953.1 372.2 reduce-scatter.20
  1328.2 372.4 reduce-scatter.22
  1880.4 83.1 all-gather.11
  1966.9 87.7 all-gather.9
  2058.2 87.2 all-gather.13
where the time goes:
time: 2180 us
  waiting for transfers between devices  1080 us (50%)
  blocking collectives  628 us (29%)
  matrix products  312 us (14%)
  other arithmetic  60.5 us (3%)
  local copies, waits for them, and re-layouts  47.2 us (2%)
  starting transfers between devices  29.9 us (1%)
    unnamed x23, waiting for transfers between devices  821 us
    unnamed x1, blocking collectives  455 us
    reshape x3, waiting for transfers between devices, step(): t.reshape(-1, *t.shape[2:])  258 us
    reduce_sum x1, blocking collectives, of_a_group(): jnp.sum(g * g)  173 us
    dot_general x5, matrix products, layer(): gate = jnp.dot(a, w['w_gate'], preferred_element_type=jnp.float32)  108 us
    dot_general x5, matrix products, layer(): up = jnp.dot(a, w['w_up'], preferred_element_type=jnp.float32)  106 us
    dot_general x5, matrix products, matmul(): jnp.dot(a, w, preferred_element_type=jnp.float32).astype(jnp.bfloat16)  97.5 us
    unnamed x7, other arithmetic  45.9 us
  transfers between devices with their start and end apart: 19, of which 6 were waited for; matrix products, arithmetic and copies ran while one was open for 32% of the time, Pallas kernels for 0%

commit v1 on v0

v1 whole, which is shorter than its diff:
```python
import jax
import jax.numpy as jnp
from jax import lax
from jax.experimental import pallas as pl
from jax.experimental.pallas import tpu as pltpu
from jax.sharding import PartitionSpec as P

NAMES = ("w_gate", "w_up", "w_down")
BF16, F32 = jnp.bfloat16, jnp.float32
MESH = pl.DeviceIdType.MESH
VMEM_LIMIT = 63 * 1024 * 1024
WIDE, DEEP = "wide", "deep"
ROWS = {WIDE: 64, DEEP: 176}
WINDOW = {WIDE: 16, DEEP: 48}
COLUMNS = {WIDE: 2816, DEEP: 1024}
JOBS = {
    WIDE: ((0, 1, 0, 512), (0, -1, 512, 384), (1, 1, 896, 384), (1, -1, 1280, 512), (2, 1, 1792, 512), (2, -1, 2304, 512)),
    DEEP: ((0, 1, 0, 256), (0, -1, 256, 128), (1, 1, 384, 128), (1, -1, 512, 256), (2, 1, 768, 128), (2, -1, 896, 128)),
}
COLOURS = {
    WIDE: ((0, 0, 896), (1, 896, 896), (2, 1792, 1024)),
    DEEP: ((0, 0, 384), (1, 384, 384), (2, 768, 256)),
}


def coordinates():
    i = lax.axis_index("dp")
    return [lax.div(i, 16), lax.rem(lax.div(i, 4), 4), lax.rem(i, 4)]


def at(axis, by):
    c = coordinates()
    c[axis] = lax.rem(c[axis] + by + 4, 4)
    return {"dp": c[0] * 16 + c[1] * 4 + c[2]}


def place(axis, by):
    return lax.rem(coordinates()[axis] + by + 4, 4)


def greet(offsets):
    barrier = pltpu.get_barrier_semaphore()
    for axis, by in offsets:
        pl.semaphore_signal(barrier, inc=1, device_id=at(axis, by), device_id_type=MESH)
    pl.semaphore_wait(barrier, len(offsets))


NEXT = tuple((axis, by) for axis in range(3) for by in (1, -1))


def first_row(form, z):
    if form == WIDE:
        return pl.multiple_of(z * 16, 8)
    return pl.multiple_of(lax.div(z, 2) * 88 + lax.rem(z, 2) * 40, 8)


def part(form, axis, k):
    index = [slice(None)] * 3
    index[axis] = pl.ds(first_row(form, k), WINDOW[form]) if axis == 2 else pl.ds(k, 1)
    return tuple(index)


def extent(form, done):
    return (1 if 0 in done else 4, 1 if 1 in done else 4, WINDOW[form] if 2 in done else ROWS[form])


class Scratch:
    def __init__(self):
        self.shapes = []

    def new(self, shape, dtype):
        self.shapes.append(pltpu.VMEM(shape, dtype))
        return len(self.shapes) - 1


class Copies:
    def __init__(self):
        self.count = 0

    def new(self):
        self.count += 1
        return self.count - 1


def each(shape, body):
    def step(t, _):
        body(lax.div(t, shape[1]), lax.rem(t, shape[1]))
        return 0

    lax.fori_loop(0, shape[0] * shape[1], step, 0)


class SumJob:
    def __init__(self, form, job, scratch, remote, local):
        self.form = form
        self.colour, self.d, self.first, self.width = job
        self.axes = [(self.colour + n) % 3 for n in range(3)]
        done = []
        self.phases = []
        for n, axis in enumerate(self.axes):
            done.append(axis)
            shape = (*extent(form, done), self.width)
            names = {}
            for name in ("r1", "ro", "rm", "sm"):
                names[name] = scratch.new(shape, BF16)
            if n == 0:
                names["own"] = scratch.new(shape, BF16)
                names["l1"], names["l0"] = local.new(), local.new()
            else:
                names["s1"] = scratch.new(shape, BF16)
                names["so"] = scratch.new(shape, BF16)
            if n < 2:
                names["acc"] = scratch.new(shape, F32)
            for name in ("c1", "co", "cm"):
                names[name] = remote.new()
            self.phases.append((axis, shape, names))

    def bind(self, source, out, squares, refs, send, recv, local):
        self.source, self.out, self.squares = source, out, squares
        self.refs, self.send, self.recv, self.local = refs, send, recv, local

    def buf(self, n, name):
        return self.refs[self.phases[n][2][name]]

    def copy(self, n, which):
        axis, _, names = self.phases[n]
        d = self.d
        target, by = {"c1": ("r1", d), "co": ("ro", -d), "cm": ("rm", d)}[which]
        if which == "cm":
            source = self.buf(n, "sm")
        elif n == 0:
            k = place(axis, 2 if which == "c1" else -d)
            source = self.source.at[(*part(self.form, axis, k), pl.ds(self.first, self.width))]
        else:
            source = self.buf(n, "s1" if which == "c1" else "so")
        number = names[which]
        return pltpu.make_async_remote_copy(
            src_ref=source,
            dst_ref=self.buf(n, target),
            send_sem=self.send.at[number],
            recv_sem=self.recv.at[number],
            device_id=at(axis, by),
            device_id_type=MESH,
        )

    def load(self, which):
        axis, _, names = self.phases[0]
        k = place(axis, self.d if which == "l1" else 0)
        return pltpu.make_async_copy(
            self.source.at[(*part(self.form, axis, k), pl.ds(self.first, self.width))],
            self.buf(0, "sm" if which == "l1" else "own"),
            self.local.at[names[which]],
        )

    def rows(self, n, k):
        axis = self.phases[n][0]
        acc = self.buf(n - 1, "acc")

        def read(i, j):
            if axis == 0:
                return acc[k, j]
            if axis == 1:
                return acc[i, k]
            return acc[i, j, pl.ds(first_row(self.form, k), WINDOW[self.form]), :]

        return read

    def begin(self, n):
        axis, shape, _ = self.phases[n]
        if n == 0:
            self.copy(0, "c1").start()
            self.load("l1").start()
            self.copy(0, "co").start()
            self.load("l0").start()
            return
        for name, by, copy in (("s1", 2, "c1"), ("so", -self.d, "co")):
            read, buf = self.rows(n, place(axis, by)), self.buf(n, name)

            def body(i, j):
                buf[i, j] = read(i, j).astype(BF16)

            each(shape, body)
            self.copy(n, copy).start()

    def middle(self, n):
        axis, shape, _ = self.phases[n]
        r1, sm = self.buf(n, "r1"), self.buf(n, "sm")
        if n == 0:
            self.load("l1").wait()
            read = lambda i, j: sm[i, j].astype(F32)
        else:
            read = self.rows(n, place(axis, self.d))
        self.copy(n, "c1").wait_recv()

        def body(i, j):
            sm[i, j] = (read(i, j) + r1[i, j].astype(F32)).astype(BF16)

        each(shape, body)
        self.copy(n, "cm").start()

    def end(self, n):
        axis, shape, _ = self.phases[n]
        rm, ro = self.buf(n, "rm"), self.buf(n, "ro")
        if n == 0:
            self.load("l0").wait()
            own = self.buf(0, "own")
            read = lambda i, j: own[i, j].astype(F32)
        else:
            read = self.rows(n, place(axis, 0))
        self.copy(n, "co").wait_recv()
        self.copy(n, "cm").wait_recv()

        def total(i, j):
            return read(i, j) + rm[i, j].astype(F32) + ro[i, j].astype(F32)

        if n < 2:
            acc = self.buf(n, "acc")

            def body(i, j):
                acc[i, j] = total(i, j)

            each(shape, body)
            return
        g = total(0, 0).astype(BF16)
        self.out[:, pl.ds(self.first, self.width)] = g
        square = g.astype(F32)
        square = square * square
        if self.form == DEEP:
            row = lax.broadcasted_iota(jnp.int32, square.shape, 0) - 4 * lax.rem(coordinates()[2], 2)
            square = jnp.where((row >= 0) & (row < 44), square, 0.0)
        square = jnp.sum(square, axis=0, keepdims=True)
        for t in range(self.width // 128):
            self.squares[...] += square[:, 128 * t : 128 * (t + 1)]

    def sent(self):
        for n in range(3):
            for which in ("c1", "co", "cm"):
                self.copy(n, which).wait_send()

    def actions(self):
        yield lambda: self.begin(0)
        yield lambda: self.middle(0)
        for n in (1, 2):

            def turn(n=n):
                self.end(n - 1)
                self.begin(n)

            yield turn
            yield lambda n=n: self.middle(n)

        def last():
            self.end(2)
            self.sent()

        yield last


def sum_kernel(forms, number):
    scratch, remote, local = Scratch(), Copies(), Copies()
    jobs = [[SumJob(form, job, scratch, remote, local) for job in JOBS[form]] for form in forms]

    def kernel(*refs):
        sources, refs = refs[: len(forms)], refs[len(forms) :]
        outs, squares, refs = refs[: len(forms)], refs[len(forms)], refs[len(forms) + 1 :]
        send, recv, loc = refs[-3:]
        greet(NEXT)
        squares[...] = jnp.zeros_like(squares)
        order = []
        for m, of_matrix in enumerate(jobs):
            for j, job in enumerate(of_matrix):
                job.bind(sources[m], outs[m], squares, refs[:-3], send, recv, loc)
                for stage, action in enumerate(job.actions()):
                    order.append((stage + 1.5 * m, m, stage, j, action))
        for *_, action in sorted(order, key=lambda o: o[:4]):
            action()

    def call(*terms):
        *sums, squares = pl.pallas_call(
            kernel,
            out_shape=[jax.ShapeDtypeStruct((WINDOW[f], COLUMNS[f]), BF16) for f in forms] + [jax.ShapeDtypeStruct((1, 128), F32)],
            in_specs=[pl.BlockSpec(memory_space=pl.ANY)] * len(forms),
            out_specs=[pl.BlockSpec(memory_space=pltpu.VMEM)] * (len(forms) + 1),
            scratch_shapes=[
                *scratch.shapes,
                pltpu.SemaphoreType.DMA((remote.count,)),
                pltpu.SemaphoreType.DMA((remote.count,)),
                pltpu.SemaphoreType.DMA((local.count,)),
            ],
            compiler_params=pltpu.CompilerParams(collective_id=number, has_side_effects=True, vmem_limit_bytes=VMEM_LIMIT),
            name=f"sum_{number}",
        )(*(t.reshape(4, 4, ROWS[f], COLUMNS[f]) for t, f in zip(terms, forms, strict=True)))
        return sums, squares

    return call


def norm_kernel(number):
    around = (1, -1, 2)

    def kernel(own, out, got, total, send, recv):
        greet(tuple((axis, by) for axis in range(3) for by in around))
        total[0] = own[...]
        for axis in range(3):
            copies = [
                pltpu.make_async_remote_copy(
                    src_ref=total.at[axis],
                    dst_ref=got.at[axis, n],
                    send_sem=send.at[axis, n],
                    recv_sem=recv.at[axis, n],
                    device_id=at(axis, by),
                    device_id_type=MESH,
                )
                for n, by in enumerate(around)
            ]
            for copy in copies:
                copy.start()
            for copy in copies:
                copy.wait_recv()
            total[axis + 1] = (total[axis] + got[axis, 2]) + (got[axis, 0] + got[axis, 1])
            for copy in copies:
                copy.wait_send()
        out[...] = total[3]

    return pl.pallas_call(
        kernel,
        out_shape=jax.ShapeDtypeStruct((8, 128), F32),
        in_specs=[pl.BlockSpec(memory_space=pltpu.VMEM)],
        out_specs=pl.BlockSpec(memory_space=pltpu.VMEM),
        scratch_shapes=[
            pltpu.VMEM((3, 3, 8, 128), F32),
            pltpu.VMEM((4, 8, 128), F32),
            pltpu.SemaphoreType.DMA((3, 3)),
            pltpu.SemaphoreType.DMA((3, 3)),
        ],
        compiler_params=pltpu.CompilerParams(collective_id=number, has_side_effects=True),
        name="norm",
    )


class GatherJob:
    def __init__(self, form, colour, remote, local):
        self.form = form
        self.colour, self.first, self.width = colour
        self.axes = [(self.colour + n) % 3 for n in range(3)]
        self.numbers = [[remote.new() for _ in range(4)] for _ in range(3)]
        self.local_number = local.new()

    def bind(self, own, out, send, recv, local):
        self.own, self.out, self.send, self.recv, self.local = own, out, send, recv, local

    def held(self, n, by, layer=None):
        index = []
        for axis in range(3):
            if axis in self.axes[:n]:
                index.append(slice(None))
                continue
            k = place(axis, by if axis == self.axes[n] else 0)
            window = WINDOW[self.form]
            index.append(pl.ds(pl.multiple_of(k * window, 8), window) if axis == 2 else pl.ds(k, 1))
        layers = slice(None) if layer is None else pl.ds(layer, 1)
        return self.out.at[(layers, *index, pl.ds(self.first, self.width))]

    def copy(self, n, which):
        axis, number = self.axes[n], self.numbers[n][which]
        if which < 2:
            by = (1, -1)[which]
            source = self.own.at[:, :, :, :, pl.ds(self.first, self.width)] if n == 0 else self.held(n, 0)
            target = self.held(n, 0)
        else:
            by = (1, -1)[which - 2]
            source = target = self.held(n, -by, which - 2)
        return pltpu.make_async_remote_copy(
            src_ref=source,
            dst_ref=target,
            send_sem=self.send.at[number],
            recv_sem=self.recv.at[number],
            device_id=at(axis, by),
            device_id_type=MESH,
        )

    def keep(self):
        return pltpu.make_async_copy(
            self.own.at[:, :, :, :, pl.ds(self.first, self.width)], self.held(0, 0), self.local.at[self.local_number]
        )

    def actions(self):
        for n in range(3):

            def begin(n=n):
                if n == 0:
                    self.keep().start()
                else:
                    self.copy(n - 1, 2).wait_recv()
                    self.copy(n - 1, 3).wait_recv()
                if n == 1:
                    self.keep().wait()
                self.copy(n, 0).start()
                self.copy(n, 1).start()

            def forward(n=n):
                self.copy(n, 0).wait_recv()
                self.copy(n, 2).start()
                self.copy(n, 1).wait_recv()
                self.copy(n, 3).start()

            yield begin
            yield forward

        def last():
            self.copy(2, 2).wait_recv()
            self.copy(2, 3).wait_recv()
            for n in range(3):
                for which in range(4):
                    self.copy(n, which).wait_send()

        yield last


def gather_kernel(forms, number):
    remote, local = Copies(), Copies()
    jobs = [[GatherJob(form, colour, remote, local) for colour in COLOURS[form]] for form in forms]

    def kernel(*refs):
        owns, outs = refs[: len(forms)], refs[len(forms) : 2 * len(forms)]
        send, recv, loc = refs[2 * len(forms) :]
        greet(NEXT)
        order = []
        for m, of_matrix in enumerate(jobs):
            for j, job in enumerate(of_matrix):
                job.bind(owns[m], outs[m], send, recv, loc)
                for stage, action in enumerate(job.actions()):
                    order.append((stage, m, j, action))
        for *_, action in sorted(order, key=lambda o: o[:3]):
            action()

    def call(*owns):
        return pl.pallas_call(
            kernel,
            out_shape=[jax.ShapeDtypeStruct((2, 4, 4, 4 * WINDOW[f], COLUMNS[f]), BF16) for f in forms],
            in_specs=[pl.BlockSpec(memory_space=pltpu.VMEM)] * len(forms),
            out_specs=[pl.BlockSpec(memory_space=pl.ANY)] * len(forms),
            scratch_shapes=[
                pltpu.SemaphoreType.DMA((remote.count,)),
                pltpu.SemaphoreType.DMA((remote.count,)),
                pltpu.SemaphoreType.DMA((local.count,)),
            ],
            compiler_params=pltpu.CompilerParams(collective_id=number, has_side_effects=True),
            name="gather",
        )(*(o.reshape(2, 1, 1, WINDOW[f], COLUMNS[f]) for o, f in zip(owns, forms, strict=True)))

    return call


def matmul(a, w):
    return jnp.dot(a, w, preferred_element_type=F32).astype(BF16)


def normed(h):
    wide = h.astype(F32)
    scale = lax.rsqrt(jnp.mean(wide**2, -1, keepdims=True) + 1e-6)
    return (wide * scale).astype(BF16)


def layer(h, w):
    a = normed(h)
    gate = jnp.dot(a, w["w_gate"], preferred_element_type=F32)
    up = jnp.dot(a, w["w_up"], preferred_element_type=F32)
    return h + matmul((jax.nn.silu(gate) * up).astype(BF16), w["w_down"])


def adamw(w, m, v, g):
    m = 0.9 * m + 0.1 * g
    v = 0.95 * v + 0.05 * g * g
    step = m * lax.rsqrt(v + 1e-8) + 0.1 * w
    return (w - 0.02 * step).astype(BF16), m, v


def stack(weights, h):
    for w in weights:
        h = layer(h, w)
    return h


def solution(mesh):
    def step(x, dy, *arrays):
        weights, m, v = (arrays[i : i + 3] for i in (0, 3, 6))
        x, dy = x[0], dy[0]
        by_layer = [{name: w[n] for name, w in zip(NAMES, weights, strict=True)} for n in range(2)]
        _, back = jax.vjp(lambda w: stack(w, x), by_layer)
        terms = back(dy)[0]
        z = lax.rem(lax.axis_index("dp"), 4)
        gate, up, down, squares = [None] * 2, [None] * 2, [None] * 2, []
        (down[1], down[0]), s = sum_kernel((DEEP, DEEP), 0)(terms[1]["w_down"], terms[0]["w_down"])
        squares.append(s)
        for n in (1, 0):
            (gate[n], up[n]), s = sum_kernel((WIDE, WIDE), 1 + n)(terms[n]["w_gate"], terms[n]["w_up"])
            squares.append(s)
        down = [lax.dynamic_slice_in_dim(d, 4 * lax.rem(z, 2), 44, 0) for d in down]
        gradients = [jnp.stack(g).astype(F32) for g in (gate, up, down)]
        squares = jnp.broadcast_to(sum(jnp.sum(s) for s in squares), (8, 128))
        total = norm_kernel(3)(squares)[0, 0]
        factor = jnp.minimum(1.0, 0.5 * lax.rsqrt(total / (6 * 1024 * 2816) + 1e-30))
        new = []
        for w, m_, v_, g in zip(weights, m, v, gradients, strict=True):
            rows = g.shape[1]
            own = lax.dynamic_slice_in_dim(w, lax.axis_index("dp") * rows, rows, 1)
            new.append(adamw(own.astype(F32), m_, v_, g * factor))
        own = [one[0] for one in new]
        own[2] = jnp.pad(own[2], ((0, 0), (0, 4), (0, 0)))
        gate, up, down = gather_kernel((WIDE, WIDE, DEEP), 4)(*own)
        down = down.reshape(2, 64, 48, 1024)[:, :, :44].reshape(2, 2816, 1024)
        return (
            gate.reshape(2, 1024, 2816),
            up.reshape(2, 1024, 2816),
            down,
            *(one[1] for one in new),
            *(one[2] for one in new),
        )

    whole, rows = P(None, None, None), P(None, "dp", None)
    tokens, out, out_rows = P(("rep", "dp"), None, None), P("rep", None, None), P("rep", "dp", None)
    return jax.shard_map(
        step,
        mesh=mesh,
        in_specs=(tokens, tokens, *[whole] * 3, *[rows] * 6),
        out_specs=(*[out] * 3, *[out_rows] * 6),
        check_vma=False,
    )
```

time: 2180 us -> 722 us (0.33)
  waiting for transfers between devices: 1080 us -> 0 us
  blocking collectives: 628 us -> 0 us
  Pallas kernels: 0 us -> 311 us
  other arithmetic: 60.5 us -> 17.4 us
  starting transfers between devices: 29.9 us -> 0 us
    unnamed x23 -> x0, waiting for transfers between devices: 821 us -> none
    unnamed x1 -> x0, blocking collectives: 455 us -> none
    pallas_call x0 -> x5, Pallas kernels: none -> 311 us  [the longest x3 177 us: call(): pl.pallas_call(kernel, out_shape=[jax.ShapeDtypeStruct((WINDOW[f], COLUMN...]
    reshape x3 -> x0, waiting for transfers between devices: 258 us -> none  [step(): t.reshape(-1, *t.shape[2:])]
    reduce_sum x1 -> x0, blocking collectives: 173 us -> none  [of_a_group(): jnp.sum(g * g)]
    unnamed x7 -> x2, other arithmetic: 45.9 us -> 0.01 us
    unnamed x16 -> x0, starting transfers between devices: 29.8 us -> none
    unnamed x55 -> x44, local copies, waits for them, and re-layouts: 45.7 us -> 56.6 us
  transfers between devices with their start and end apart: 19 -> 0, of which waited for: 6 -> 0; matrix products, arithmetic and copies ran while one was open for 32% -> 0% of each run, Pallas kernels for 0% -> 0%
where the time goes in v1:
time: 722 us; the launch traced here: 715 us
  matrix products  324 us (45%)
  Pallas kernels  311 us (43%)
  local copies, waits for them, and re-layouts  59.1 us (8%)
  other arithmetic  17.4 us (2%)
    pallas_call x3, Pallas kernels, call(): pl.pallas_call(kernel, out_shape=[jax.ShapeDtypeStruct((WINDOW[f], COLUMN...  177 us
    pallas_call x1, Pallas kernels, call(): pl.pallas_call(kernel, out_shape=[jax.ShapeDtypeStruct((2, 4, 4, 4 * WIND...  117 us
    dot_general x5, matrix products, layer(): gate = jnp.dot(a, w['w_gate'], preferred_element_type=F32)  113 us
    dot_general x5, matrix products, layer(): up = jnp.dot(a, w['w_up'], preferred_element_type=F32)  113 us
    dot_general x5, matrix products, matmul(): return jnp.dot(a, w, preferred_element_type=F32).astype(BF16)  97.9 us
    unnamed x44, local copies, waits for them, and re-layouts  56.6 us
    pallas_call x1, Pallas kernels, step(): total = norm_kernel(3)(squares)[0, 0]  16 us

profile of v1, /device:TPU:0, one launch (start us, length us, event | category | flops | bytes accessed | tf_op | source)
XLA Modules:
  0.0 715.0 jit_solution(16295044828395607391)
XLA Ops:
  0.6 6.5 copy.27
  7.2 3.1 fusion.15
  10.2 0.0 copy-start.10
  10.2 19.9 %fusion.35 = f32[2048,2816]{1,0:T(8,128)} fusion(bf16[2,1024,2816]{2,1,0:T(8,128)(2,1)} %param.13, bf16[1,2048,1024]{2,1,0:T(8,128)(2,1)} %param.11, f32[2048]{0:T(1024)S(1)} %add_rsqrt_fusion), kind=kOutput, calls=%fused_computation.54 | convolution fusion | flops 11817451520 | bytes 33038336 | tf_op jit(solution)/shard_map/jvp()/dot_general | solution.py:467
  30.1 0.0 copy-done.10
  30.1 28.7 %multiply_convert_fusion.1 = (bf16[2048,2816]{1,0:T(8,128)(2,1)}, f32[2048,2816]{1,0:T(8,128)}) fusion(f32[2048,2816]{1,0:T(8,128)} %fusion.35, bf16[2,1024,2816]{2,1,0:T(8,128)(2,1)} %param.14, bf16[1,2048,1024]{2,1,0:T(8,128)(2,1)} %param.11, f32[2048]{0:T(1024)S(1)} %add_rsqrt_fusion), kind=kOutput, calls=%fused_computation.17 | convolution fusion | flops 11852054528 | bytes 67641344 | tf_op jit(solution)/shard_map/jvp()/dot_general | solution.py:468
  58.8 19.9 %fusion.19 = (f32[2048]{0:T(1024)S(1)}, bf16[2048,1024]{0,1:T(8,128)(2,1)}) fusion(bf16[2048,2816]{1,0:T(8,128)(2,1)} %get-tuple-element.60, bf16[2,2816,1024]{2,1,0:T(8,128)(2,1)} %param.15, bf16[1,2048,1024]{1,2,0:T(8,128)(2,1)} %copy.27), kind=kOutput, calls=%fused_computation.37 | convolution fusion | flops 11821643776 | bytes 25698304 | tf_op jit(solution)/shard_map/jvp()/dot_general | solution.py:456
  78.7 0.6 copy-done.8
  79.3 20.2 %fusion.22 = f32[2048,2816]{1,0:T(8,128)} fusion(bf16[2,1024,2816]{2,1,0:T(8,128)(2,1)} %param.14, bf16[2048,1024]{0,1:T(8,128)(2,1)} %get-tuple-element.63, f32[2048]{0:T(1024)S(1)} %fusion.84), kind=kOutput, calls=%fused_computation.41 | convolution fusion | flops 11817451520 | bytes 33038336 | tf_op jit(solution)/shard_map/jvp()/dot_general | solution.py:468
  99.5 0.0 copy-done.3
  99.5 17.3 %convolution_convert_fusion.1 = bf16[2048,2816]{1,0:T(8,128)(2,1)} fusion(bf16[2,2816,1024]{2,1,0:T(8,128)(2,1)} %param.15, bf16[1,2048,1024]{2,1,0:T(8,128)(2,1)S(1)} %copy-done.3), kind=kOutput, calls=%fused_computation.29 | convolution fusion | flops 11816927232 | bytes 21495808 | tf_op jit(solution)/shard_map/transpose(jvp())/dot_general | solution.py:456
  116.8 0.0 copy-done.1
  116.8 31.8 %fusion.2 = (bf16[2048,2816]{1,0:T(8,128)(2,1)}, f32[2048,2816]{1,0:T(8,128)}) fusion(f32[2048,2816]{1,0:T(8,128)} %fusion.22, bf16[2048,2816]{1,0:T(8,128)(2,1)} %convolution_convert_fusion.1, bf16[2,1024,2816]{2,1,0:T(8,128)(2,1)} %param.13, bf16[2048,1024]{0,1:T(8,128)(2,1)S(1)} %copy-done.1, f32[2048]{0:T(1024)S(1)} %fusion.84), kind=kOutput, calls=%fused_computation.8 | convolution fusion | flops 11886657536 | bytes 79175680 | tf_op jit(solution)/shard_map/jvp()/dot_general | solution.py:467
  148.5 23.6 %fusion.40 = bf16[2816,1024]{1,0:T(8,128)(2,1)} fusion(f32[2048,2816]{1,0:T(8,128)} %fusion.22, bf16[1,2048,1024]{2,1,0:T(8,128)(2,1)} %param.12, f32[2048,2816]{1,0:T(8,128)} %get-tuple-element.65), kind=kOutput, calls=%fused_computation.59 | convolution fusion | flops 11848646656 | bytes 56098816 | tf_op jit(solution)/shard_map/transpose(jvp())/dot_general | solution.py:456
  172.1 18.9 %fusion.12 = bf16[2048,1024]{0,1:T(8,128)(2,1)S(1)} fusion(bf16[2048,2816]{1,0:T(8,128)(2,1)} %convolution_convert_fusion.1, bf16[2,1024,2816]{2,1,0:T(8,128)(2,1)} %param.14, f32[2048,2816]{1,0:T(8,128)} %get-tuple-element.65), kind=kOutput, calls=%fused_computation.21 | convolution fusion | flops 11845763072 | bytes 44564480 | tf_op jit(solution)/shard_map/transpose(jvp())/dot_general | solution.py:468
  191.0 0.0 copy-start.9
  191.0 18.4 %fusion.21 = (f32[2048]{0:T(1024)S(1)}, bf16[2048,1024]{0,1:T(8,128)(2,1)}) fusion(bf16[2048,1024]{0,1:T(8,128)(2,1)S(1)} %copy-done.1, bf16[2048,1024]{0,1:T(8,128)(2,1)S(1)} %fusion.12, bf16[2048,2816]{1,0:T(8,128)(2,1)} %get-tuple-element.64, bf16[2,1024,2816]{2,1,0:T(8,128)(2,1)} %param.13), kind=kOutput, calls=%fused_computation.39 | convolution fusion | flops 11821643776 | bytes 29892608 | tf_op jit(solution)/shard_map/transpose(jvp())/dot_general | solution.py:467
  209.5 6.5 copy.28
  216.0 0.0 copy-done.9
  216.0 6.2 fusion.53
  222.2 0.0 copy-start.2
  222.2 18.3 %convolution_convert_fusion.2 = bf16[2816,1024]{1,0:T(8,128)(2,1)} fusion(bf16[2048,2816]{1,0:T(8,128)(2,1)} %get-tuple-element.60, bf16[2048,1024]{0,1:T(8,128)(2,1)S(1)} %fusion.53), kind=kOutput, calls=%fused_computation.63 | convolution fusion | flops 11814043648 | bytes 21495808 | tf_op jit(solution)/shard_map/transpose(jvp())/dot_general | solution.py:456
  240.5 0.0 copy-done.2
  240.5 69.9 %sum_0.1 = (bf16[48,1024]{1,0:T(8,128)(2,1)}, bf16[48,1024]{1,0:T(8,128)(2,1)}, f32[1,128]{1,0:T(1,128)}) custom-call(bf16[4,4,176,1024]{3,2,1,0:T(8,128)(2,1)} %bitcast.98, bf16[4,4,176,1024]{3,2,1,0:T(8,128)(2,1)} %bitcast.103), custom_call_target="tpu_custom_call" | custom-call | tf_op jit(solution)/shard_map/sum_0/pallas_call | solution.py:279
  310.4 1.2 reduce_sum.61
  311.6 18.5 %convolution_convert_fusion.3 = bf16[1024,2816]{1,0:T(8,128)(2,1)} fusion(bf16[2048,2816]{1,0:T(8,128)(2,1)} %get-tuple-element.64, bf16[2048,1024]{0,1:T(8,128)(2,1)} %get-tuple-element.63, f32[2048]{0:T(1024)S(1)} %fusion.84), kind=kOutput, calls=%fused_computation.64 | convolution fusion | flops 11817451520 | bytes 21504000 | tf_op jit(solution)/shard_map/transpose(jvp())/dot_general | solution.py:467
  330.2 22.5 %fusion.41 = bf16[1024,2816]{1,0:T(8,128)(2,1)} fusion(bf16[2048,2816]{1,0:T(8,128)(2,1)} %convolution_convert_fusion.1, bf16[2048,1024]{0,1:T(8,128)(2,1)} %get-tuple-element.63, f32[2048]{0:T(1024)S(1)} %fusion.84, f32[2048,2816]{1,0:T(8,128)} %get-tuple-element.65), kind=kOutput, calls=%fused_computation.60 | convolution fusion | flops 11854938112 | bytes 44572672 | tf_op jit(solution)/shard_map/transpose(jvp())/dot_general | solution.py:468
  352.7 54.9 %sum_2.1 = (bf16[16,2816]{1,0:T(8,128)(2,1)}, bf16[16,2816]{1,0:T(8,128)(2,1)}, f32[1,128]{1,0:T(1,128)}) custom-call(bf16[4,4,64,2816]{3,2,1,0:T(8,128)(2,1)} %bitcast.99, bf16[4,4,64,2816]{3,2,1,0:T(8,128)(2,1)} %bitcast.101), custom_call_target="tpu_custom_call" | custom-call | tf_op jit(solution)/shard_map/sum_2/pallas_call | solution.py:279
  407.7 1.2 reduce_sum.62
  410.2 0.0 copy-start
  410.2 0.0 copy-start.11
  410.2 18.8 %convolution_convert_fusion = bf16[2048,2816]{1,0:T(8,128)(2,1)} fusion(bf16[2048,1024]{0,1:T(8,128)(2,1)} %copy-done.2, bf16[2,2816,1024]{2,1,0:T(8,128)(2,1)} %param.15), kind=kOutput, calls=%fused_computation.28 | convolution fusion | flops 11816927232 | bytes 21495808 | tf_op jit(solution)/shard_map/transpose(jvp())/dot_general | solution.py:456
  429.0 0.0 copy-done
  429.0 0.0 copy-done.11
  429.0 24.6 %fusion.42 = bf16[1024,2816]{1,0:T(8,128)(2,1)} fusion(f32[2048,2816]{1,0:T(8,128)} %fusion.35, f32[2048,2816]{1,0:T(8,128)} %get-tuple-element.61, bf16[2048,2816]{1,0:T(8,128)(2,1)} %convolution_convert_fusion, bf16[1,2048,1024]{1,2,0:T(8,128)(2,1)S(1)} %copy-done, f32[2048]{0:T(1024)S(1)} %copy-done.11), kind=kOutput, calls=%fused_computation.61 | convolution fusion | flops 11883773952 | bytes 67641344 | tf_op jit(solution)/shard_map/transpose(jvp())/dot_general | solution.py:467
  453.7 22.5 %fusion.45 = bf16[1024,2816]{1,0:T(8,128)(2,1)} fusion(bf16[2048,2816]{1,0:T(8,128)(2,1)} %convolution_convert_fusion, f32[2048,2816]{1,0:T(8,128)} %fusion.35, bf16[1,2048,1024]{1,2,0:T(8,128)(2,1)} %copy.27, f32[2048]{0:T(1024)S(1)} %copy-done.11), kind=kOutput, calls=%fused_computation.62 | convolution fusion | flops 11854938112 | bytes 44572672 | tf_op jit(solution)/shard_map/transpose(jvp())/dot_general | solution.py:468
  476.2 0.0 copy-start.7
  476.2 52.5 %sum_1.1 = (bf16[16,2816]{1,0:T(8,128)(2,1)}, bf16[16,2816]{1,0:T(8,128)(2,1)}, f32[1,128]{1,0:T(1,128)}) custom-call(bf16[4,4,64,2816]{3,2,1,0:T(8,128)(2,1)} %bitcast.100, bf16[4,4,64,2816]{3,2,1,0:T(8,128)(2,1)} %bitcast.102), custom_call_target="tpu_custom_call" | custom-call | tf_op jit(solution)/shard_map/sum_1/pallas_call | solution.py:279
  528.7 1.2 reduce_sum.63
  530.6 0.6 broadcast_in_dim.2.own
  531.2 16.0 %norm.1 = f32[8,128]{1,0:T(8,128)} custom-call(f32[8,128]{1,0:T(8,128)} %broadcast_in_dim.2.own), custom_call_target="tpu_custom_call" | custom-call | tf_op jit(solution)/shard_map/norm/pallas_call | solution.py:502
  547.2 1.2 slice.30
  549.1 0.0 copy-done.4
  549.1 2.8 fusion.82
  551.9 0.0 copy-done.7
  551.9 0.1 dynamic-slice_bitcast_fusion
  552.0 1.6 fusion.71
  553.6 0.7 pad_bitcast_fusion.refs_2_
  554.3 117.5 %gather.1 = (bf16[2,4,4,64,2816]{4,3,2,1,0:T(8,128)(2,1)}, bf16[2,4,4,64,2816]{4,3,2,1,0:T(8,128)(2,1)}, bf16[2,4,4,192,1024]{4,3,2,1,0:T(8,128)(2,1)}) custom-call(bf16[2,1,1,16,2816]{4,3,2,1,0:T(8,128)(2,1)} %get-tuple-element.68.refs_0_, bf16[2,1,1,16,2816]{4,3,2,1,0:T(8,128)(2,1)} %get-tuple-element.54.refs_1_, ...), custom_call_target="tpu_custom_call" | custom-call | tf_op jit(solution)/shard_map/gather/pallas_call | solution.py:438
  671.8 0.0 slice-start.3
  671.8 0.0 slice-start.4
  671.8 20.4 %copy.36 = bf16[2,64,44,1024]{3,0,2,1:T(2,128)(2,1)S(1)} copy(bf16[2,64,44,1024]{3,2,1,0:T(8,128)(2,1)} %bitcast.91) | data formatting | bytes 23068672
  692.3 0.0 slice-start.5
  692.3 8.1 %copy.33 = bf16[2,2816,1024]{2,1,0:T(8,128)(2,1)} copy(bf16[2,2816,1024]{2,0,1:T(2,128)(2,1)S(1)} %bitcast.90) | data formatting | bytes 23068672
  700.4 1.0 copy.34
  701.4 1.0 copy.35
  702.4 0.0 slice-done.3
  702.5 0.0 slice-done.5
  702.5 0.0 slice-start.1
  702.5 0.0 slice-start.2
  702.5 5.8 copy.47
  708.3 0.7 slice-done.1
  709.0 1.3 slice-done.2
  710.3 4.4 copy.48
  (16 shorter events, 0.0 us)
Async XLA Ops:
  10.2 19.9 %copy-start.10 = (f32[2048]{0:T(1024)}, f32[2048]{0:T(1024)S(1)}, u32[]{:S(2)}) copy-start(f32[2048]{0:T(1024)S(1)} %add_rsqrt_fusion) | copy-start | bytes 24580
  78.7 0.6 copy-start.8
  79.3 20.2 %copy-start.3 = (bf16[1,2048,1024]{2,1,0:T(8,128)(2,1)S(1)}, bf16[1,2048,1024]{2,1,0:T(8,128)(2,1)}, u32[]{:S(2)}) copy-start(bf16[1,2048,1024]{2,1,0:T(8,128)(2,1)} %param.12) | copy-start | bytes 12582916
  99.5 17.3 %copy-start.1 = (bf16[2048,1024]{0,1:T(8,128)(2,1)S(1)}, bf16[2048,1024]{0,1:T(8,128)(2,1)}, u32[]{:S(2)}) copy-start(bf16[2048,1024]{0,1:T(8,128)(2,1)} %get-tuple-element.63) | copy-start | bytes 12582916
  191.0 25.0 %copy-start.9 = (f32[2048]{0:T(1024)S(1)}, f32[2048]{0:T(1024)}, u32[]{:S(2)}) copy-start(f32[2048]{0:T(1024)} %copy-done.8) | copy-start | bytes 24580
  222.2 18.3 %copy-start.2 = (bf16[2048,1024]{0,1:T(8,128)(2,1)}, bf16[2048,1024]{0,1:T(8,128)(2,1)S(1)}, u32[]{:S(2)}) copy-start(bf16[2048,1024]{0,1:T(8,128)(2,1)S(1)} %fusion.53) | copy-start | bytes 12582916
  410.2 18.9 %copy-start = (bf16[1,2048,1024]{1,2,0:T(8,128)(2,1)S(1)}, bf16[1,2048,1024]{1,2,0:T(8,128)(2,1)}, u32[]{:S(2)}) copy-start(bf16[1,2048,1024]{1,2,0:T(8,128)(2,1)} %copy.27) | copy-start | bytes 12582916
  410.2 18.9 %copy-start.11 = (f32[2048]{0:T(1024)S(1)}, f32[2048]{0:T(1024)}, u32[]{:S(2)}) copy-start(f32[2048]{0:T(1024)} %copy-done.10) | copy-start | bytes 24580
  476.2 72.9 %copy-start.4 = (f32[2,16,2816]{2,1,0:T(8,128)S(1)}, f32[2,16,2816]{2,1,0:T(8,128)}, u32[]{:S(2)}) copy-start(f32[2,16,2816]{2,1,0:T(8,128)} %param.20) | copy-start | bytes 1081348
  476.2 72.9 %copy-start.5 = (f32[2,16,2816]{2,1,0:T(8,128)S(1)}, f32[2,16,2816]{2,1,0:T(8,128)}, u32[]{:S(2)}) copy-start(f32[2,16,2816]{2,1,0:T(8,128)} %param.17) | copy-start | bytes 1081348
  476.2 75.7 %copy-start.6 = (bf16[48,1024]{1,0:T(8,128)(2,1)S(1)}, bf16[48,1024]{1,0:T(8,128)(2,1)}, u32[]{:S(2)}) copy-start(bf16[48,1024]{1,0:T(8,128)(2,1)} %get-tuple-element.29) | copy-start | bytes 294916
  476.2 75.7 %copy-start.7 = (bf16[48,1024]{1,0:T(8,128)(2,1)S(1)}, bf16[48,1024]{1,0:T(8,128)(2,1)}, u32[]{:S(2)}) copy-start(bf16[48,1024]{1,0:T(8,128)(2,1)} %get-tuple-element.28) | copy-start | bytes 294916
  671.8 30.7 %slice-start.3 = ((s8[11534336]{0:T(1024)(128)(4,1)}), s8[4194304]{0:T(1024)(128)(4,1)S(1)}, s32[]{:S(2)}) async-start(s8[11534336]{0:T(1024)(128)(4,1)} %bitcast.95), calls=%async_computation.3 | async-start | bytes 8388608
  671.8 30.7 %slice-start.4 = ((s8[11534336]{0:T(1024)(128)(4,1)}), s8[4194304]{0:T(1024)(128)(4,1)S(1)}, s32[]{:S(2)}) async-start(s8[11534336]{0:T(1024)(128)(4,1)} %bitcast.95), calls=%async_computation.4 | async-start | bytes 8388608
  692.3 10.2 %slice-start.5 = ((s8[11534336]{0:T(1024)(128)(4,1)}), s8[3145728]{0:T(1024)(128)(4,1)S(1)}, s32[]{:S(2)}) async-start(s8[11534336]{0:T(1024)(128)(4,1)} %bitcast.95), calls=%async_computation.5 | async-start | bytes 6291456
  701.4 6.9 slice-start
  702.5 6.6 slice-start.1
  702.5 7.8 %slice-start.2 = ((s8[11534336]{0:T(1024)(128)(4,1)}), s8[3145728]{0:T(1024)(128)(4,1)S(1)}, s32[]{:S(2)}) async-start(s8[11534336]{0:T(1024)(128)(4,1)} %bitcast.92), calls=%async_computation.2 | async-start | bytes 6291456

commit v2 on v1

--- a/solution.py
+++ b/solution.py
@@ -1,3 +1,5 @@
+import functools
+
 import jax
 import jax.numpy as jnp
 from jax import lax
@@ -6,17 +8,24 @@
 from jax.sharding import PartitionSpec as P
 
 NAMES = ("w_gate", "w_up", "w_down")
+AXES = range(3)
+PAIR = pltpu.SemaphoreType.DMA((2,))
 BF16, F32 = jnp.bfloat16, jnp.float32
 MESH = pl.DeviceIdType.MESH
-VMEM_LIMIT = 63 * 1024 * 1024
+VMEM_LIMIT, SMALL_LIMIT = 63 << 20, 8 << 20
+TOKENS, D, FF = 2048, 1024, 2816
 WIDE, DEEP = "wide", "deep"
 ROWS = {WIDE: 64, DEEP: 176}
 WINDOW = {WIDE: 16, DEEP: 48}
-COLUMNS = {WIDE: 2816, DEEP: 1024}
-JOBS = {
-    WIDE: ((0, 1, 0, 512), (0, -1, 512, 384), (1, 1, 896, 384), (1, -1, 1280, 512), (2, 1, 1792, 512), (2, -1, 2304, 512)),
-    DEEP: ((0, 1, 0, 256), (0, -1, 256, 128), (1, 1, 384, 128), (1, -1, 512, 256), (2, 1, 768, 128), (2, -1, 896, 128)),
-}
+COLUMNS = {WIDE: FF, DEEP: D}
+TILE = 256
+TILES = FF // TILE
+GATE = tuple((n % 3, 1 - 2 * (n // 3 % 2), TILE * (n + min(n, 4)), 2 * TILE if n < 4 else TILE) for n in range(7))
+UP = tuple(((c + 1) % 3, -d, first, width) for c, d, first, width in GATE)
+DOWN = ((0, 1, 0, 256), (0, -1, 256, 128), (1, 1, 384, 128), (1, -1, 512, 128), (2, 1, 640, 128), (2, -1, 768, 256))
+SECOND_DOWN, SECOND_WIDE = (0, 5, 12, 18, 20, 26, 82), (0, 6, 10, 13, 27, 36, 77)
+FIRST_DOWN, FIRST_WIDE = (0, 5, 10, 13, 18, 20, 32), (0, 3, 6, 9, 12, 22, 39)
+READY = (2, 4, 6, 8, 9, 10, 11)
 COLOURS = {
     WIDE: ((0, 0, 896), (1, 896, 896), (2, 1792, 1024)),
     DEEP: ((0, 0, 384), (1, 384, 384), (2, 768, 256)),
@@ -45,7 +54,7 @@
     pl.semaphore_wait(barrier, len(offsets))
 
 
-NEXT = tuple((axis, by) for axis in range(3) for by in (1, -1))
+NEXT = tuple((axis, by) for axis in AXES for by in (1, -1))
 
 
 def first_row(form, z):
@@ -94,7 +103,7 @@
     def __init__(self, form, job, scratch, remote, local):
         self.form = form
         self.colour, self.d, self.first, self.width = job
-        self.axes = [(self.colour + n) % 3 for n in range(3)]
+        self.axes = [(self.colour + n) % 3 for n in AXES]
         done = []
         self.phases = []
         for n, axis in enumerate(self.axes):
@@ -104,7 +113,6 @@
             for name in ("r1", "ro", "rm", "sm"):
                 names[name] = scratch.new(shape, BF16)
             if n == 0:
-                names["own"] = scratch.new(shape, BF16)
                 names["l1"], names["l0"] = local.new(), local.new()
             else:
                 names["s1"] = scratch.new(shape, BF16)
@@ -148,7 +156,7 @@
         k = place(axis, self.d if which == "l1" else 0)
         return pltpu.make_async_copy(
             self.source.at[(*part(self.form, axis, k), pl.ds(self.first, self.width))],
-            self.buf(0, "sm" if which == "l1" else "own"),
+            self.buf(0, "sm" if which == "l1" else "r1"),
             self.local.at[names[which]],
         )
 
@@ -171,7 +179,6 @@
             self.copy(0, "c1").start()
             self.load("l1").start()
             self.copy(0, "co").start()
-            self.load("l0").start()
             return
         for name, by, copy in (("s1", 2, "c1"), ("so", -self.d, "co")):
             read, buf = self.rows(n, place(axis, by)), self.buf(n, name)
@@ -197,13 +204,15 @@
 
         each(shape, body)
         self.copy(n, "cm").start()
+        if n == 0:
+            self.load("l0").start()
 
     def end(self, n):
         axis, shape, _ = self.phases[n]
         rm, ro = self.buf(n, "rm"), self.buf(n, "ro")
         if n == 0:
             self.load("l0").wait()
-            own = self.buf(0, "own")
+            own = self.buf(0, "r1")
             read = lambda i, j: own[i, j].astype(F32)
         else:
             read = self.rows(n, place(axis, 0))
@@ -233,7 +242,7 @@
             self.squares[...] += square[:, 128 * t : 128 * (t + 1)]
 
     def sent(self):
-        for n in range(3):
+        for n in AXES:
             for which in ("c1", "co", "cm"):
                 self.copy(n, which).wait_send()
 
@@ -256,94 +265,424 @@
         yield last
 
 
-def sum_kernel(forms, number):
-    scratch, remote, local = Scratch(), Copies(), Copies()
-    jobs = [[SumJob(form, job, scratch, remote, local) for job in JOBS[form]] for form in forms]
-
-    def kernel(*refs):
-        sources, refs = refs[: len(forms)], refs[len(forms) :]
-        outs, squares, refs = refs[: len(forms)], refs[len(forms)], refs[len(forms) + 1 :]
-        send, recv, loc = refs[-3:]
-        greet(NEXT)
-        squares[...] = jnp.zeros_like(squares)
-        order = []
-        for m, of_matrix in enumerate(jobs):
-            for j, job in enumerate(of_matrix):
-                job.bind(sources[m], outs[m], squares, refs[:-3], send, recv, loc)
-                for stage, action in enumerate(job.actions()):
-                    order.append((stage + 1.5 * m, m, stage, j, action))
-        for *_, action in sorted(order, key=lambda o: o[:4]):
-            action()
-
-    def call(*terms):
-        *sums, squares = pl.pallas_call(
-            kernel,
-            out_shape=[jax.ShapeDtypeStruct((WINDOW[f], COLUMNS[f]), BF16) for f in forms] + [jax.ShapeDtypeStruct((1, 128), F32)],
-            in_specs=[pl.BlockSpec(memory_space=pl.ANY)] * len(forms),
-            out_specs=[pl.BlockSpec(memory_space=pltpu.VMEM)] * (len(forms) + 1),
-            scratch_shapes=[
-                *scratch.shapes,
-                pltpu.SemaphoreType.DMA((remote.count,)),
-                pltpu.SemaphoreType.DMA((remote.count,)),
-                pltpu.SemaphoreType.DMA((local.count,)),
-            ],
-            compiler_params=pltpu.CompilerParams(collective_id=number, has_side_effects=True, vmem_limit_bytes=VMEM_LIMIT),
-            name=f"sum_{number}",
-        )(*(t.reshape(4, 4, ROWS[f], COLUMNS[f]) for t, f in zip(terms, forms, strict=True)))
-        return sums, squares
-
-    return call
-
-
-def norm_kernel(number):
-    around = (1, -1, 2)
-
-    def kernel(own, out, got, total, send, recv):
-        greet(tuple((axis, by) for axis in range(3) for by in around))
-        total[0] = own[...]
-        for axis in range(3):
-            copies = [
-                pltpu.make_async_remote_copy(
-                    src_ref=total.at[axis],
-                    dst_ref=got.at[axis, n],
-                    send_sem=send.at[axis, n],
-                    recv_sem=recv.at[axis, n],
-                    device_id=at(axis, by),
-                    device_id_type=MESH,
-                )
-                for n, by in enumerate(around)
-            ]
+class Sums:
+    def __init__(self, matrices):
+        self.scratch, self.remote, self.local = Scratch(), Copies(), Copies()
+        self.forms = [form for form, *_ in matrices]
+        self.jobs = []
+        for m, (form, jobs, begins, later) in enumerate(matrices):
+            for job, begin in zip(jobs, begins, strict=True):
+                self.jobs.append((m, SumJob(form, job, self.scratch, self.remote, self.local), [begin + n for n in later]))
+        self.out_shape = [jax.ShapeDtypeStruct((WINDOW[f], COLUMNS[f]), BF16) for f in self.forms]
+        self.out_shape.append(jax.ShapeDtypeStruct((1, 128), F32))
+        self.scratch_shapes = [
+            *self.scratch.shapes,
+            pltpu.SemaphoreType.DMA((self.remote.count,)),
+            pltpu.SemaphoreType.DMA((self.remote.count,)),
+            pltpu.SemaphoreType.DMA((self.local.count,)),
+        ]
+
+    def run(self, step, steps, parts, sources, outs, refs):
+        *outs, squares = outs
+        *refs, send, recv, local = refs
+        due, end = {}, steps * parts
+        for j, (m, job, times) in enumerate(self.jobs):
+            job.bind(sources[m], outs[m], squares, refs, send, recv, local)
+            for stage, (time, action) in enumerate(zip(times, job.actions(), strict=True)):
+                due.setdefault(min(time, end), []).append((time, stage, j, action))
+
+        def now(time):
+            for *_, action in sorted(due.get(time, ()), key=lambda o: o[:3]):
+                action()
+
+        def reach(part):
+            for time in range(part, end, parts):
+                if time in due:
+                    pl.when(step == time // parts)(functools.partial(now, time))
+
+        def rest():
+            pl.when(step == steps - 1)(functools.partial(now, end))
+
+        def enter(offsets):
+            @pl.when(step == 0)
+            def _():
+                greet(offsets)
+                squares[...] = jnp.zeros_like(squares)
+
+        return enter, reach, rest
+
+
+def dot(a, b, dims=((1,), (0,))):
+    return lax.dot_general(a, b, (dims, ((), ())), preferred_element_type=F32)
+
+
+NT, TN = ((1,), (1,)), ((0,), (0,))
+BLOCK = 1024
+
+
+def blocks(n, size, body):
+    lax.fori_loop(0, n // size, lambda t, _: (body(pl.ds(pl.multiple_of(t * size, size), size)), 0)[1], 0)
+
+
+def kept(shape):
+    return pl.BlockSpec(shape, lambda i: (0,) * len(shape), pipeline_mode=pl.Buffered(1))
+
+
+def wide_tile(number, turn=lambda i: i):
+    return pl.BlockSpec((None, D, TILE), lambda i: (number, 0, turn(i)))
+
+
+def deep_tile(number):
+    return pl.BlockSpec((None, TILE, D), lambda i: (number, i, 0))
+
+
+def columns_tile(turn=lambda i: i):
+    return pl.BlockSpec((TOKENS, TILE), lambda i: (0, turn(i)))
+
+
+ANY = pl.BlockSpec(memory_space=pl.ANY)
+VMEM = pl.BlockSpec(memory_space=pltpu.VMEM)
+
+
+def normed_block(wide):
+    return (wide * lax.rsqrt(jnp.mean(wide * wide, -1, keepdims=True) + 1e-6)).astype(BF16)
+
+
+def first_layer(x, w_gate, w_up, w_down):
+    def kernel(x, wg, wu, wd, gate, up, s, a1t, h1, a2, a2t, a_s, h_s, t_s, acc, sem):
+        i = pl.program_id(0)
+
+        def put(n, source, target):
+            return pltpu.make_async_copy(source, target, sem.at[n])
+
+        @pl.when(i == 0)
+        def _():
+            def body(rows):
+                a = normed_block(x[rows, :].astype(F32))
+                a_s[rows, :] = a
+                t_s[:, rows] = a.T
+                acc[rows, :] = jnp.zeros((TILE, D), F32)
+
+            blocks(TOKENS, TILE, body)
+            put(0, t_s, a1t).start()
+
+        def body(rows):
+            a = a_s[rows, :]
+            g = dot(a, wg[...])
+            u = dot(a, wu[...])
+            gate[rows, :] = g
+            up[rows, :] = u
+            p = (g * lax.logistic(g) * u).astype(BF16)
+            s[rows, :] = p
+            acc[rows, :] += dot(p, wd[...])
+
+        blocks(TOKENS, BLOCK, body)
+
+        @pl.when(i == TILES - 1)
+        def _():
+            put(0, t_s, a1t).wait()
+
+            def body(rows):
+                h = x[rows, :] + acc[rows, :].astype(BF16)
+                h_s[rows, :] = h
+                a = normed_block(h.astype(F32))
+                a_s[rows, :] = a
+                t_s[:, rows] = a.T
+
+            blocks(TOKENS, TILE, body)
+            copies = [put(0, t_s, a2t), put(1, h_s, h1), put(2, a_s, a2)]
             for copy in copies:
                 copy.start()
             for copy in copies:
-                copy.wait_recv()
-            total[axis + 1] = (total[axis] + got[axis, 2]) + (got[axis, 0] + got[axis, 1])
-            for copy in copies:
-                copy.wait_send()
-        out[...] = total[3]
-
+                copy.wait()
+
+    tokens, turned = jax.ShapeDtypeStruct((TOKENS, D), BF16), jax.ShapeDtypeStruct((D, TOKENS), BF16)
+    hidden = (TOKENS, FF)
     return pl.pallas_call(
         kernel,
-        out_shape=jax.ShapeDtypeStruct((8, 128), F32),
-        in_specs=[pl.BlockSpec(memory_space=pltpu.VMEM)],
-        out_specs=pl.BlockSpec(memory_space=pltpu.VMEM),
+        grid=(TILES,),
+        out_shape=[
+            jax.ShapeDtypeStruct(hidden, F32),
+            jax.ShapeDtypeStruct(hidden, F32),
+            jax.ShapeDtypeStruct(hidden, BF16),
+            turned,
+            tokens,
+            tokens,
+            turned,
+        ],
+        in_specs=[kept((TOKENS, D)), wide_tile(0), wide_tile(0), deep_tile(0)],
+        out_specs=[columns_tile()] * 3 + [ANY] * 4,
         scratch_shapes=[
-            pltpu.VMEM((3, 3, 8, 128), F32),
-            pltpu.VMEM((4, 8, 128), F32),
-            pltpu.SemaphoreType.DMA((3, 3)),
-            pltpu.SemaphoreType.DMA((3, 3)),
+            pltpu.VMEM((TOKENS, D), BF16),
+            pltpu.VMEM((TOKENS, D), BF16),
+            pltpu.VMEM((D, TOKENS), BF16),
+            pltpu.VMEM((TOKENS, D), F32),
+            pltpu.SemaphoreType.DMA((3,)),
         ],
-        compiler_params=pltpu.CompilerParams(collective_id=number, has_side_effects=True),
-        name="norm",
+        compiler_params=pltpu.CompilerParams(vmem_limit_bytes=VMEM_LIMIT),
+        name="first_layer",
+    )(x, w_gate, w_up, w_down)
+
+
+def through_product(ds, g, u):
+    sig = lax.logistic(g)
+    silu = g * sig
+    return (ds * u * (sig + silu * (1.0 - sig))).astype(BF16), (ds * silu).astype(BF16)
+
+
+def second_layer(a2, dy, w_gate, w_up, w_down):
+    def kernel(a2, dy, wg, wu, wd, dg, du, dwd, s):
+        def body(rows):
+            a = a2[rows, :]
+            g = dot(a, wg[...])
+            u = dot(a, wu[...])
+            ds = dot(dy[rows, :], wd[...], NT).astype(BF16).astype(F32)
+            s[rows, :] = (g * lax.logistic(g) * u).astype(BF16)
+            dg[rows, :], du[rows, :] = through_product(ds, g, u)
+
+        blocks(TOKENS, BLOCK, body)
+        dwd[...] = dot(s[...], dy[...], TN).astype(BF16)
+
+    return pl.pallas_call(
+        kernel,
+        grid=(TILES,),
+        out_shape=[jax.ShapeDtypeStruct((TOKENS, FF), BF16)] * 2 + [jax.ShapeDtypeStruct((FF, D), BF16)],
+        in_specs=[kept((TOKENS, D))] * 2 + [wide_tile(1), wide_tile(1), deep_tile(1)],
+        out_specs=[columns_tile()] * 2 + [pl.BlockSpec((TILE, D), lambda i: (i, 0))],
+        scratch_shapes=[pltpu.VMEM((TOKENS, TILE), BF16)],
+        compiler_params=pltpu.CompilerParams(vmem_limit_bytes=VMEM_LIMIT),
+        name="second_layer",
+    )(a2, dy, w_gate, w_up, w_down)
+
+
+def down_term(s, dy, da2, h1):
+    def kernel(s, dy, da2, h1, out, dh, dh_s, sem):
+        copy = pltpu.make_async_copy(dh_s, dh, sem)
+
+        @pl.when(pl.program_id(0) == 0)
+        def _():
+            def body(rows):
+                dh_s[rows, :] = through_norm(dy[rows, :], da2[rows, :], h1[rows, :])
+
+            blocks(TOKENS, TILE, body)
+            copy.start()
+
+        out[...] = dot(s[...], dh_s[...], TN).astype(BF16)
+        pl.when(pl.program_id(0) == TILES - 1)(copy.wait)
+
+    return pl.pallas_call(
+        kernel,
+        grid=(TILES,),
+        out_shape=[jax.ShapeDtypeStruct((FF, D), BF16), jax.ShapeDtypeStruct((TOKENS, D), BF16)],
+        in_specs=[columns_tile()] + [kept((TOKENS, D))] * 3,
+        out_specs=[pl.BlockSpec((TILE, D), lambda i: (i, 0)), ANY],
+        scratch_shapes=[pltpu.VMEM((TOKENS, D), BF16), pltpu.SemaphoreType.DMA(())],
+        compiler_params=pltpu.CompilerParams(vmem_limit_bytes=VMEM_LIMIT),
+        name="down_term",
+    )(s, dy, da2, h1)
+
+
+def store_terms(at, dg, du, stage_g, stage_u):
+    for stage, cotangent in ((stage_g, dg), (stage_u, du)):
+        stage[...] = dot(at[...], cotangent[...]).astype(BF16).reshape(stage.shape)
+
+
+class Terms:
+    def __init__(self, stages, terms, sem):
+        self.stages, self.terms, self.sem = stages, terms, sem
+
+    def copies(self, tile):
+        columns = pl.ds(pl.multiple_of(tile * TILE, TILE), TILE)
+        return [
+            pltpu.make_async_copy(stage, term.at[:, :, :, columns], self.sem.at[n])
+            for n, (stage, term) in enumerate(zip(self.stages, self.terms, strict=True))
+        ]
+
+    def start(self, tile):
+        for copy in self.copies(tile):
+            copy.start()
+
+    def wait(self, tile):
+        for copy in self.copies(tile):
+            copy.wait()
+
+
+TERM = jax.ShapeDtypeStruct((4, 4, 64, FF), BF16)
+STAGES = [pltpu.VMEM((4, 4, 64, TILE), BF16)] * 2 + [PAIR]
+
+
+def second_sums(a2t, dg, du, w_gate, w_up, down, number):
+    steps = 2 * TILES
+    sums = Sums(
+        (
+            (DEEP, DOWN, (0,) * 6, SECOND_DOWN),
+            (WIDE, GATE, READY, SECOND_WIDE),
+            (WIDE, UP, READY, SECOND_WIDE),
+        )
     )
+
+    def kernel(a2t, dg, du, wg, wu, down, *refs):
+        outs, refs = refs[:4], refs[4:]
+        da2, term_g, term_u, stage_g, stage_u, term_sem, acc, half, half_sem, *refs = refs
+        i = pl.program_id(0)
+        terms = Terms((stage_g, stage_u), (term_g, term_u), term_sem)
+        enter, reach, rest = sums.run(i, steps, 1, (down, term_g, term_u), outs, refs)
+        enter(NEXT)
+
+        @pl.when((i > 0) & (i <= TILES))
+        def _():
+            terms.wait(i - 1)
+
+        reach(0)
+
+        @pl.when(i < TILES)
+        def _():
+            store_terms(a2t, dg, du, stage_g, stage_u)
+            terms.start(i)
+
+        @pl.when(i == TILES)
+        def _():
+            blocks(TOKENS, TILE, lambda rows: acc.__setitem__((rows, slice(None)), jnp.zeros((TILE, D), F32)))
+
+        @pl.when(i >= TILES)
+        def _():
+            def body(rows):
+                acc[rows, :] += dot(dg[rows, :], wg[...], NT) + dot(du[rows, :], wu[...], NT)
+
+            blocks(TOKENS, BLOCK, body)
+
+        @pl.when(i == steps - 1)
+        def _():
+            for n in range(4):
+                rows = pl.ds(512 * n, 512)
+                copy = pltpu.make_async_copy(half.at[n % 2], da2.at[rows, :], half_sem.at[n % 2])
+                if n >= 2:
+                    copy.wait()
+                half[n % 2] = acc[rows, :].astype(BF16)
+                copy.start()
+            for n in (2, 3):
+                pltpu.make_async_copy(half.at[n % 2], da2.at[pl.ds(512 * n, 512), :], half_sem.at[n % 2]).wait()
+
+        rest()
+
+    turn = lambda i: lax.rem(i, TILES)
+    late = lambda i: jnp.maximum(i - TILES, 0)
+    d, g, u, squares, da2, *_ = pl.pallas_call(
+        kernel,
+        grid=(steps,),
+        out_shape=[*sums.out_shape, jax.ShapeDtypeStruct((TOKENS, D), BF16), TERM, TERM],
+        in_specs=[kept((D, TOKENS)), columns_tile(turn), columns_tile(turn), wide_tile(1, late), wide_tile(1, late), ANY],
+        out_specs=[VMEM] * 4 + [ANY] * 3,
+        scratch_shapes=[
+            *STAGES,
+            pltpu.VMEM((TOKENS, D), F32),
+            pltpu.VMEM((2, 512, D), BF16),
+            PAIR,
+            *sums.scratch_shapes,
+        ],
+        compiler_params=pltpu.CompilerParams(collective_id=number, has_side_effects=True, vmem_limit_bytes=VMEM_LIMIT),
+        name="second_sums",
+    )(a2t, dg, du, w_gate, w_up, down.reshape(4, 4, 176, D))
+    return d, g, u, squares, da2
+
+
+def first_sums(a1t, dh, gate, up, w_down, down, others, number):
+    steps = TILES
+    sums = Sums(
+        (
+            (DEEP, DOWN, (0,) * 6, FIRST_DOWN),
+            (WIDE, GATE, [2 * n for n in READY], FIRST_WIDE),
+            (WIDE, UP, [2 * n for n in READY], FIRST_WIDE),
+        )
+    )
+
+    def kernel(a1t, dh, gate, up, wd, down, others, *refs):
+        outs, refs = refs[:4], refs[4:]
+        total, term_g, term_u, stage_g, stage_u, term_sem, dg, du, *refs = refs
+        *refs, got, held, norm_send, norm_recv = refs
+        i = pl.program_id(0)
+        terms = Terms((stage_g, stage_u), (term_g, term_u), term_sem)
+        enter, reach, rest = sums.run(i, steps, 2, (down, term_g, term_u), outs, refs)
+        enter([(axis, by) for axis in AXES for by in AROUND])
+
+        @pl.when(i > 0)
+        def _():
+            terms.wait(i - 1)
+
+        reach(0)
+
+        def body(rows):
+            ds = dot(dh[rows, :], wd[...], NT).astype(BF16).astype(F32)
+            dg[rows, :], du[rows, :] = through_product(ds, gate[rows, :], up[rows, :])
+
+        blocks(TOKENS, BLOCK, body)
+        reach(1)
+        store_terms(a1t, dg, du, stage_g, stage_u)
+        terms.start(i)
+
+        @pl.when(i == steps - 1)
+        def _():
+            terms.wait(i)
+
+        rest()
+
+        @pl.when(i == steps - 1)
+        def _():
+            norm(jnp.sum(outs[3][...] + others[...]), total, got, held, norm_send, norm_recv)
+
+    d, g, u, _, total, *_ = pl.pallas_call(
+        kernel,
+        grid=(steps,),
+        out_shape=[*sums.out_shape, jax.ShapeDtypeStruct(SCALAR, F32), TERM, TERM],
+        in_specs=[kept((D, TOKENS)), kept((TOKENS, D)), columns_tile(), columns_tile(), deep_tile(0), ANY, VMEM],
+        out_specs=[VMEM] * 5 + [ANY] * 2,
+        scratch_shapes=[*STAGES, pltpu.VMEM((TOKENS, TILE), BF16), pltpu.VMEM((TOKENS, TILE), BF16), *sums.scratch_shapes, *NORM],
+        compiler_params=pltpu.CompilerParams(collective_id=number, has_side_effects=True, vmem_limit_bytes=VMEM_LIMIT),
+        name="first_sums",
+    )(a1t, dh, gate, up, w_down, down.reshape(4, 4, 176, D), others)
+    return d, g, u, total
+
+
+AROUND = (1, -1, 2)
+SCALAR = (8, 128)
+NORM = [
+    pltpu.VMEM((3, 3, *SCALAR), F32),
+    pltpu.VMEM((4, *SCALAR), F32),
+    pltpu.SemaphoreType.DMA((3, 3)),
+    pltpu.SemaphoreType.DMA((3, 3)),
+]
+
+
+def norm(own, out, got, held, send, recv):
+    held[0] = jnp.full(SCALAR, own, F32)
+    for axis in AXES:
+        copies = [
+            pltpu.make_async_remote_copy(
+                src_ref=held.at[axis],
+                dst_ref=got.at[axis, n],
+                send_sem=send.at[axis, n],
+                recv_sem=recv.at[axis, n],
+                device_id=at(axis, by),
+                device_id_type=MESH,
+            )
+            for n, by in enumerate(AROUND)
+        ]
+        for copy in copies:
+            copy.start()
+        for copy in copies:
+            copy.wait_recv()
+        held[axis + 1] = (held[axis] + got[axis, 2]) + (got[axis, 0] + got[axis, 1])
+        for copy in copies:
+            copy.wait_send()
+    out[...] = held[3]
 
 
 class GatherJob:
     def __init__(self, form, colour, remote, local):
         self.form = form
         self.colour, self.first, self.width = colour
-        self.axes = [(self.colour + n) % 3 for n in range(3)]
-        self.numbers = [[remote.new() for _ in range(4)] for _ in range(3)]
+        self.axes = [(self.colour + n) % 3 for n in AXES]
+        self.numbers = [[remote.new() for _ in range(4)] for _ in AXES]
         self.local_number = local.new()
 
     def bind(self, own, out, send, recv, local):
@@ -351,7 +690,7 @@
 
     def held(self, n, by, layer=None):
         index = []
-        for axis in range(3):
+        for axis in AXES:
             if axis in self.axes[:n]:
                 index.append(slice(None))
                 continue
@@ -385,7 +724,7 @@
         )
 
     def actions(self):
-        for n in range(3):
+        for n in AXES:
 
             def begin(n=n):
                 if n == 0:
@@ -410,7 +749,7 @@
         def last():
             self.copy(2, 2).wait_recv()
             self.copy(2, 3).wait_recv()
-            for n in range(3):
+            for n in AXES:
                 for which in range(4):
                     self.copy(n, which).wait_send()
 
@@ -437,36 +776,71 @@
     def call(*owns):
         return pl.pallas_call(
             kernel,
-            out_shape=[jax.ShapeDtypeStruct((2, 4, 4, 4 * WINDOW[f], COLUMNS[f]), BF16) for f in forms],
-            in_specs=[pl.BlockSpec(memory_space=pltpu.VMEM)] * len(forms),
-            out_specs=[pl.BlockSpec(memory_space=pl.ANY)] * len(forms),
+            out_shape=[pltpu.VMEM((2, 4, 4, 4 * WINDOW[f], COLUMNS[f]), BF16) for f in forms],
+            in_specs=[VMEM] * len(forms),
+            out_specs=[VMEM] * len(forms),
             scratch_shapes=[
                 pltpu.SemaphoreType.DMA((remote.count,)),
                 pltpu.SemaphoreType.DMA((remote.count,)),
                 pltpu.SemaphoreType.DMA((local.count,)),
             ],
-            compiler_params=pltpu.CompilerParams(collective_id=number, has_side_effects=True),
+            compiler_params=pltpu.CompilerParams(collective_id=number, has_side_effects=True, vmem_limit_bytes=SMALL_LIMIT),
             name="gather",
         )(*(o.reshape(2, 1, 1, WINDOW[f], COLUMNS[f]) for o, f in zip(owns, forms, strict=True)))
 
     return call
 
 
-def matmul(a, w):
-    return jnp.dot(a, w, preferred_element_type=F32).astype(BF16)
-
-
-def normed(h):
-    wide = h.astype(F32)
+def settle(gate, up, down):
+    def kernel(gate, up, down, gate_out, up_out, down_out, wide, close, sem, close_sem):
+        copies = [pltpu.make_async_copy(gate, gate_out, sem.at[0]), pltpu.make_async_copy(up, up_out, sem.at[1])]
+        for copy in copies:
+            copy.start()
+
+        def put(t):
+            return pltpu.make_async_copy(
+                close.at[lax.rem(t, 2)], down_out.at[lax.div(t, 16), lax.rem(t, 16)], close_sem.at[lax.rem(t, 2)]
+            )
+
+        def step(t, _):
+            @pl.when(t >= 2)
+            def _():
+                put(t - 2).wait()
+
+            for z in range(4):
+                block = down[lax.div(t, 16), lax.rem(t, 16), pl.ds(48 * z, 48), :]
+                wide[pl.ds(44 * z, 48), :] = block.astype(F32)
+            close[lax.rem(t, 2)] = wide[pl.ds(0, 176), :].astype(BF16)
+            put(t).start()
+            return 0
+
+        lax.fori_loop(0, 32, step, 0)
+        put(30).wait()
+        put(31).wait()
+        for copy in copies:
+            copy.wait()
+
+    return pl.pallas_call(
+        kernel,
+        out_shape=[jax.ShapeDtypeStruct(gate.shape, BF16)] * 2 + [jax.ShapeDtypeStruct((2, 16, 176, D), BF16)],
+        in_specs=[VMEM] * 3,
+        out_specs=[ANY] * 3,
+        scratch_shapes=[
+            pltpu.VMEM((184, D), F32),
+            pltpu.VMEM((2, 176, D), BF16),
+            PAIR,
+            PAIR,
+        ],
+        compiler_params=pltpu.CompilerParams(vmem_limit_bytes=SMALL_LIMIT),
+        name="settle",
+    )(gate, up, down.reshape(2, 16, 192, D))
+
+
+def through_norm(dy, da, h):
+    wide, da = h.astype(F32), da.astype(F32)
     scale = lax.rsqrt(jnp.mean(wide**2, -1, keepdims=True) + 1e-6)
-    return (wide * scale).astype(BF16)
-
-
-def layer(h, w):
-    a = normed(h)
-    gate = jnp.dot(a, w["w_gate"], preferred_element_type=F32)
-    up = jnp.dot(a, w["w_up"], preferred_element_type=F32)
-    return h + matmul((jax.nn.silu(gate) * up).astype(BF16), w["w_down"])
+    along = jnp.mean(da * wide, -1, keepdims=True) * scale**3
+    return dy + (da * scale - wide * along).astype(BF16)
 
 
 def adamw(w, m, v, g):
@@ -476,31 +850,21 @@
     return (w - 0.02 * step).astype(BF16), m, v
 
 
-def stack(weights, h):
-    for w in weights:
-        h = layer(h, w)
-    return h
-
-
 def solution(mesh):
     def step(x, dy, *arrays):
         weights, m, v = (arrays[i : i + 3] for i in (0, 3, 6))
         x, dy = x[0], dy[0]
-        by_layer = [{name: w[n] for name, w in zip(NAMES, weights, strict=True)} for n in range(2)]
-        _, back = jax.vjp(lambda w: stack(w, x), by_layer)
-        terms = back(dy)[0]
+        w_gate, w_up, w_down = weights
         z = lax.rem(lax.axis_index("dp"), 4)
-        gate, up, down, squares = [None] * 2, [None] * 2, [None] * 2, []
-        (down[1], down[0]), s = sum_kernel((DEEP, DEEP), 0)(terms[1]["w_down"], terms[0]["w_down"])
-        squares.append(s)
-        for n in (1, 0):
-            (gate[n], up[n]), s = sum_kernel((WIDE, WIDE), 1 + n)(terms[n]["w_gate"], terms[n]["w_up"])
-            squares.append(s)
-        down = [lax.dynamic_slice_in_dim(d, 4 * lax.rem(z, 2), 44, 0) for d in down]
+        gate1, up1, s1, a1t, h1, a2, a2t = first_layer(x, w_gate, w_up, w_down)
+        dg, du, down2 = second_layer(a2, dy, w_gate, w_up, w_down)
+        down_2, gate_2, up_2, squares_2, da2 = second_sums(a2t, dg, du, w_gate, w_up, down2, 0)
+        down1, dh = down_term(s1, dy, da2, h1)
+        down_1, gate_1, up_1, total = first_sums(a1t, dh, gate1, up1, w_down, down1, squares_2, 1)
+        gate, up = (gate_1, gate_2), (up_1, up_2)
+        down = [lax.dynamic_slice_in_dim(d, 4 * lax.rem(z, 2), 44, 0) for d in (down_1, down_2)]
         gradients = [jnp.stack(g).astype(F32) for g in (gate, up, down)]
-        squares = jnp.broadcast_to(sum(jnp.sum(s) for s in squares), (8, 128))
-        total = norm_kernel(3)(squares)[0, 0]
-        factor = jnp.minimum(1.0, 0.5 * lax.rsqrt(total / (6 * 1024 * 2816) + 1e-30))
+        factor = jnp.minimum(1.0, 0.5 * lax.rsqrt(total[0, 0] / (6 * D * FF) + 1e-30))
         new = []
         for w, m_, v_, g in zip(weights, m, v, gradients, strict=True):
             rows = g.shape[1]
@@ -508,12 +872,11 @@
             new.append(adamw(own.astype(F32), m_, v_, g * factor))
         own = [one[0] for one in new]
         own[2] = jnp.pad(own[2], ((0, 0), (0, 4), (0, 0)))
-        gate, up, down = gather_kernel((WIDE, WIDE, DEEP), 4)(*own)
-        down = down.reshape(2, 64, 48, 1024)[:, :, :44].reshape(2, 2816, 1024)
+        gate, up, down = settle(*gather_kernel((WIDE, WIDE, DEEP), 2)(*own))
         return (
-            gate.reshape(2, 1024, 2816),
-            up.reshape(2, 1024, 2816),
-            down,
+            gate.reshape(2, D, FF),
+            up.reshape(2, D, FF),
+            down.reshape(2, FF, D),
             *(one[1] for one in new),
             *(one[2] for one in new),
         )

time: 722 us -> 514 us (0.71)
  matrix products: 324 us -> 0 us
  Pallas kernels: 311 us -> 504 us
  local copies, waits for them, and re-layouts: 59.1 us -> 4.2 us
  other arithmetic: 17.4 us -> 4.3 us
    dot_general x15 -> x0, matrix products: 324 us -> none  [the longest x5 113 us: layer(): gate = jnp.dot(a, w['w_gate'], preferred_element_type=F32)]
    pallas_call x5 -> x7, Pallas kernels: 311 us -> 504 us  [the longest x1 124 us: call(): pl.pallas_call(kernel, out_shape=[pltpu.VMEM((2, 4, 4, 4 * WINDOW[f], COL...]
    unnamed x44 -> x10, local copies, waits for them, and re-layouts: 56.6 us -> 2.05 us
where the time goes in v2:
time: 514 us
  Pallas kernels  504 us (98%)
    pallas_call x1, Pallas kernels, call(): pl.pallas_call(kernel, out_shape=[pltpu.VMEM((2, 4, 4, 4 * WINDOW[f], COL...  124 us
    pallas_call x1, Pallas kernels, first_sums(): pl.pallas_call(kernel, grid=(steps,), out_shape=[*sums.out_shape, jax.Sha...  114 us
    pallas_call x1, Pallas kernels, second_sums(): pl.pallas_call(kernel, grid=(steps,), out_shape=[*sums.out_shape, jax.Sha...  105 us
    pallas_call x1, Pallas kernels, second_layer(): pl.pallas_call(kernel, grid=(TILES,), out_shape=[jax.ShapeDtypeStruct((TO...  60.2 us
    pallas_call x1, Pallas kernels, first_layer(): pl.pallas_call(kernel, grid=(TILES,), out_shape=[jax.ShapeDtypeStruct(hid...  56 us
    pallas_call x1, Pallas kernels, down_term(): pl.pallas_call(kernel, grid=(TILES,), out_shape=[jax.ShapeDtypeStruct((FF...  24 us
    pallas_call x1, Pallas kernels, settle(): pl.pallas_call(kernel, out_shape=[jax.ShapeDtypeStruct(gate.shape, BF16)]...  20.2 us

profile of v2, /device:TPU:0, one launch (start us, length us, event | category | flops | bytes accessed | tf_op | source)
XLA Modules:
  0.0 513.6 jit_solution(7599692365479979997)
XLA Ops:
  0.6 56.0 %first_layer.1 = (f32[2048,2816]{1,0:T(8,128)}, f32[2048,2816]{1,0:T(8,128)}, bf16[2048,2816]{1,0:T(8,128)(2,1)}, bf16[1024,2048]{1,0:T(8,128)(2,1)}, bf16[2048,...) custom-call(bf16[2048,1024]{1,0:T(8,128)(2,1)} %bitcast.30, bf16[2,1024,2816]{2,1,0:T(8,128)(2,1)} %wg.5, ...), custom_call_target="tpu_custom_call" | custom-call | tf_op jit(solution)/shard_map/first_layer/pallas_call | solution.py:401
  56.7 60.2 %second_layer.1 = (bf16[2048,2816]{1,0:T(8,128)(2,1)}, bf16[2048,2816]{1,0:T(8,128)(2,1)}, bf16[2816,1024]{1,0:T(8,128)(2,1)}) custom-call(bf16[2048,1024]{1,0:T(8,128)(2,1)} %get-tuple-element.39.a2, bf16[2048,1024]{1,0:T(8,128)(2,1)} %bitcast.26, bf16[2,1024,2816]{2,1,0:T(8,128)(2,1)} %wg.5, bf16[2,1024,2816]{2,1,0:T(8,128)(2,1)} %wu.5, ...), custom_call_target="tpu_custom_call" | custom-call | tf_op jit(solution)/shard_map/second_layer/pallas_call | solution.py:446
  116.9 105.0 %second_sums.1 = (bf16[48,1024]{1,0:T(8,128)(2,1)}, bf16[16,2816]{1,0:T(8,128)(2,1)}, bf16[16,2816]{1,0:T(8,128)(2,1)}, f32[1,128]{1,0:T(1,128)}, bf16[2048,1024...) custom-call(bf16[1024,2048]{1,0:T(8,128)(2,1)} %get-tuple-element.38.a2t, ...), custom_call_target="tpu_custom_call" | custom-call | tf_op jit(solution)/shard_map/second_sums/pallas_call | solution.py:570
  221.9 24.0 %down_term.1 = (bf16[2816,1024]{1,0:T(8,128)(2,1)}, bf16[2048,1024]{1,0:T(8,128)(2,1)}) custom-call(bf16[2048,2816]{1,0:T(8,128)(2,1)} %get-tuple-element.37.s, bf16[2048,1024]{1,0:T(8,128)(2,1)} %bitcast.27, bf16[2048,1024]{1,0:T(8,128)(2,1)} %get-tuple-element.43.da2, bf16[2048,1024]{1,0:T(8,128)(2,1)} %get-tuple-element.44.h1), custom_call_target="tpu_custom_call" | custom-call | tf_op jit(solution)/shard_map/down_term/pallas_call | solution.py:473
  245.9 0.0 copy-start.2
  246.0 0.0 copy-start
  246.0 0.0 copy-start.1
  246.0 0.0 copy-start.3
  246.0 114.2 %first_sums.1 = (bf16[48,1024]{1,0:T(8,128)(2,1)}, bf16[16,2816]{1,0:T(8,128)(2,1)}, bf16[16,2816]{1,0:T(8,128)(2,1)}, f32[1,128]{1,0:T(1,128)}, f32[8,128]{1,0:...) custom-call(bf16[1024,2048]{1,0:T(8,128)(2,1)} %get-tuple-element.36.a1t, ...), custom_call_target="tpu_custom_call" | custom-call | tf_op jit(solution)/shard_map/first_sums/pallas_call | solution.py:633
  360.2 0.0 copy-done.2
  360.2 0.9 dynamic-slice_bitcast_fusion
  361.1 1.2 slice.3
  363.0 0.0 copy-done
  363.0 0.0 copy-done.1
  363.0 1.4 fusion.2
  364.4 0.0 copy-done.3
  364.4 2.9 fusion.13
  367.4 124.0 %gather.1 = (bf16[2,4,4,64,2816]{4,3,2,1,0:T(8,128)(2,1)S(1)}, bf16[2,4,4,64,2816]{4,3,2,1,0:T(8,128)(2,1)S(1)}, bf16[2,4,4,192,1024]{4,3,2,1,0:T(8,128)(2,1)S(1)}) custom-call(bf16[2,1,1,16,2816]{4,3,2,1,0:T(8,128)(2,1)S(1)} %get-tuple-element.81.refs_0_, bf16[2,1,1,16,2816]{4,3,2,1,0:T(8,128)(2,1)S(1)} %get-tuple-element.75.refs_1_, ...), custom_call_target="tpu_custom_call" | custom-call | tf_op jit(solution)/shard_map/gather/pallas_call | solution.py:777
  491.4 20.2 %settle.1 = (bf16[2,4,4,64,2816]{4,3,2,1,0:T(8,128)(2,1)}, bf16[2,4,4,64,2816]{4,3,2,1,0:T(8,128)(2,1)}, bf16[2,16,176,1024]{3,2,1,0:T(8,128)(2,1)}) custom-call(bf16[2,4,4,64,2816]{4,3,2,1,0:T(8,128)(2,1)S(1)} %get-tuple-element.57.gate, bf16[2,4,4,64,2816]{4,3,2,1,0:T(8,128)(2,1)S(1)} %get-tuple-element.58.up, bf16[2,16,192,1024]{3,2,1,0:T(8,128)(2,1)S(1)} %bitcast.25), custom_call_target="tpu_custom_call" | custom-call | tf_op jit(solution)/shard_map/settle/pallas_call | solution.py:823
  511.5 1.0 copy.23
  512.6 1.0 copy.24
  (1 shorter events, 0.0 us)
Async XLA Ops:
  245.9 114.2 %copy-start.2 = (bf16[48,1024]{1,0:T(8,128)(2,1)S(1)}, bf16[48,1024]{1,0:T(8,128)(2,1)}, u32[]{:S(2)}) copy-start(bf16[48,1024]{1,0:T(8,128)(2,1)} %get-tuple-element.56) | copy-start | bytes 294916
  246.0 117.1 %copy-start = (f32[2,44,1024]{2,0,1:T(2,128)S(1)}, f32[2,44,1024]{2,0,1:T(2,128)}, u32[]{:S(2)}) copy-start(f32[2,44,1024]{2,0,1:T(2,128)} %param.21) | copy-start | bytes 1081348
  246.0 117.1 %copy-start.1 = (f32[2,44,1024]{2,0,1:T(2,128)S(1)}, f32[2,44,1024]{2,0,1:T(2,128)}, u32[]{:S(2)}) copy-start(f32[2,44,1024]{2,0,1:T(2,128)} %param.18) | copy-start | bytes 1081348
  246.0 118.4 %copy-start.3 = (bf16[16,2816]{1,0:T(8,128)(2,1)S(1)}, bf16[16,2816]{1,0:T(8,128)(2,1)}, u32[]{:S(2)}) copy-start(bf16[16,2816]{1,0:T(8,128)(2,1)} %get-tuple-element.51) | copy-start | bytes 270340

commit v3 on v2

--- a/solution.py
+++ b/solution.py
@@ -20,16 +20,23 @@
 COLUMNS = {WIDE: FF, DEEP: D}
 TILE = 256
 TILES = FF // TILE
-GATE = tuple((n % 3, 1 - 2 * (n // 3 % 2), TILE * (n + min(n, 4)), 2 * TILE if n < 4 else TILE) for n in range(7))
-UP = tuple(((c + 1) % 3, -d, first, width) for c, d, first, width in GATE)
-DOWN = ((0, 1, 0, 256), (0, -1, 256, 128), (1, 1, 384, 128), (1, -1, 512, 128), (2, 1, 640, 128), (2, -1, 768, 256))
-SECOND_DOWN, SECOND_WIDE = (0, 5, 12, 18, 20, 26, 82), (0, 6, 10, 13, 27, 36, 77)
-FIRST_DOWN, FIRST_WIDE = (0, 5, 10, 13, 18, 20, 32), (0, 3, 6, 9, 12, 22, 39)
-READY = (2, 4, 6, 8, 9, 10, 11)
+
+
+def laid(widths, kind):
+    return tuple((*kind(n), sum(widths[:n]), width) for n, width in enumerate(widths))
+
+
+WIDTHS = [2 * TILE] * 3 + [TILE] * 4 + [TILE // 2] * 2
+READY = (2, 4, 6, 7, 8, 9, 10, 11, 11)
+GATE = laid(WIDTHS, lambda n: (n % 3, 1 - 2 * (n // 3 % 2)))
+UP = laid(WIDTHS, lambda n: ((n + 1) % 3, 2 * (n // 3 % 2) - 1))
+DOWN = laid((256, 128, 128, 128, 128, 256), lambda n: (n // 2, 1 - 2 * (n % 2)))
 COLOURS = {
-    WIDE: ((0, 0, 896), (1, 896, 896), (2, 1792, 1024)),
-    DEEP: ((0, 0, 384), (1, 384, 384), (2, 768, 256)),
+    WIDE: laid((896, 896, 1024), lambda n: (n,)),
+    DEEP: laid((384, 384, 256), lambda n: (n,)),
 }
+SECOND_DOWN, SECOND_WIDE, SECOND_LATE = (0, 4, 8, 15, 17, 19, 27), (0, 3, 6, 10, 12, 13, 21), (0, 4, 6, 7, 8, 10, 14)
+FIRST_DOWN, FIRST_WIDE = (0, 5, 9, 19, 21, 42, 70), (0, 3, 8, 13, 28, 50, 69)
 
 
 def coordinates():
@@ -272,7 +279,7 @@
         self.jobs = []
         for m, (form, jobs, begins, later) in enumerate(matrices):
             for job, begin in zip(jobs, begins, strict=True):
-                self.jobs.append((m, SumJob(form, job, self.scratch, self.remote, self.local), [begin + n for n in later]))
+                self.jobs.append((m, SumJob(form, job, self.scratch, self.remote, self.local), [begin + n for n in later(begin)]))
         self.out_shape = [jax.ShapeDtypeStruct((WINDOW[f], COLUMNS[f]), BF16) for f in self.forms]
         self.out_shape.append(jax.ShapeDtypeStruct((1, 128), F32))
         self.scratch_shapes = [
@@ -317,7 +324,7 @@
 
 
 NT, TN = ((1,), (1,)), ((0,), (0,))
-BLOCK = 1024
+BLOCK, PART = 1024, 256
 
 
 def blocks(n, size, body):
@@ -455,31 +462,19 @@
     )(a2, dy, w_gate, w_up, w_down)
 
 
-def down_term(s, dy, da2, h1):
-    def kernel(s, dy, da2, h1, out, dh, dh_s, sem):
-        copy = pltpu.make_async_copy(dh_s, dh, sem)
-
-        @pl.when(pl.program_id(0) == 0)
-        def _():
-            def body(rows):
-                dh_s[rows, :] = through_norm(dy[rows, :], da2[rows, :], h1[rows, :])
-
-            blocks(TOKENS, TILE, body)
-            copy.start()
-
-        out[...] = dot(s[...], dh_s[...], TN).astype(BF16)
-        pl.when(pl.program_id(0) == TILES - 1)(copy.wait)
+def down_term(s, dh):
+    def kernel(s, dh, out):
+        out[...] = dot(s[...], dh[...], TN).astype(BF16)
 
     return pl.pallas_call(
         kernel,
         grid=(TILES,),
-        out_shape=[jax.ShapeDtypeStruct((FF, D), BF16), jax.ShapeDtypeStruct((TOKENS, D), BF16)],
-        in_specs=[columns_tile()] + [kept((TOKENS, D))] * 3,
-        out_specs=[pl.BlockSpec((TILE, D), lambda i: (i, 0)), ANY],
-        scratch_shapes=[pltpu.VMEM((TOKENS, D), BF16), pltpu.SemaphoreType.DMA(())],
+        out_shape=jax.ShapeDtypeStruct((FF, D), BF16),
+        in_specs=[columns_tile(), kept((TOKENS, D))],
+        out_specs=pl.BlockSpec((TILE, D), lambda i: (i, 0)),
         compiler_params=pltpu.CompilerParams(vmem_limit_bytes=VMEM_LIMIT),
         name="down_term",
-    )(s, dy, da2, h1)
+    )(s, dh)
 
 
 def store_terms(at, dg, du, stage_g, stage_u):
@@ -511,19 +506,20 @@
 STAGES = [pltpu.VMEM((4, 4, 64, TILE), BF16)] * 2 + [PAIR]
 
 
-def second_sums(a2t, dg, du, w_gate, w_up, down, number):
+def second_sums(a2t, dg, du, w_gate, w_up, down, dy, h1, number):
     steps = 2 * TILES
+    later = lambda begin: SECOND_LATE if begin >= 9 else SECOND_WIDE
     sums = Sums(
         (
-            (DEEP, DOWN, (0,) * 6, SECOND_DOWN),
-            (WIDE, GATE, READY, SECOND_WIDE),
-            (WIDE, UP, READY, SECOND_WIDE),
+            (DEEP, DOWN, (0,) * 6, lambda begin: SECOND_DOWN),
+            (WIDE, GATE, READY, later),
+            (WIDE, UP, READY, later),
         )
     )
 
-    def kernel(a2t, dg, du, wg, wu, down, *refs):
+    def kernel(a2t, dg, du, wg, wu, down, dy, h1, *refs):
         outs, refs = refs[:4], refs[4:]
-        da2, term_g, term_u, stage_g, stage_u, term_sem, acc, half, half_sem, *refs = refs
+        dh, term_g, term_u, stage_g, stage_u, term_sem, acc, half, half_sem, taken, taken_sem, *refs = refs
         i = pl.program_id(0)
         terms = Terms((stage_g, stage_u), (term_g, term_u), term_sem)
         enter, reach, rest = sums.run(i, steps, 1, (down, term_g, term_u), outs, refs)
@@ -551,48 +547,71 @@
 
             blocks(TOKENS, BLOCK, body)
 
+        def take(n):
+            rows = pl.ds(PART * n, PART)
+            return [
+                pltpu.make_async_copy(source.at[rows, :], taken.at[n % 2, which], taken_sem.at[n % 2, which])
+                for which, source in enumerate((dy, h1))
+            ]
+
+        def give(n):
+            return pltpu.make_async_copy(half.at[n % 2], dh.at[pl.ds(PART * n, PART), :], half_sem.at[n % 2])
+
         @pl.when(i == steps - 1)
         def _():
-            for n in range(4):
-                rows = pl.ds(512 * n, 512)
-                copy = pltpu.make_async_copy(half.at[n % 2], da2.at[rows, :], half_sem.at[n % 2])
+            parts = TOKENS // PART
+            for copy in take(0):
+                copy.start()
+            for n in range(parts):
+                if n + 1 < parts:
+                    for copy in take(n + 1):
+                        copy.start()
+                for copy in take(n):
+                    copy.wait()
                 if n >= 2:
-                    copy.wait()
-                half[n % 2] = acc[rows, :].astype(BF16)
-                copy.start()
-            for n in (2, 3):
-                pltpu.make_async_copy(half.at[n % 2], da2.at[pl.ds(512 * n, 512), :], half_sem.at[n % 2]).wait()
+                    give(n - 2).wait()
+
+                def body(rows, n=n):
+                    da = acc[pl.ds(pl.multiple_of(PART * n + rows.start, 8), rows.size), :].astype(BF16)
+                    half[n % 2, rows, :] = through_norm(taken[n % 2, 0, rows, :], da, taken[n % 2, 1, rows, :])
+
+                blocks(PART, PART // 2, body)
+                give(n).start()
+            give(parts - 2).wait()
+            give(parts - 1).wait()
 
         rest()
 
     turn = lambda i: lax.rem(i, TILES)
     late = lambda i: jnp.maximum(i - TILES, 0)
-    d, g, u, squares, da2, *_ = pl.pallas_call(
+    d, g, u, squares, dh, *_ = pl.pallas_call(
         kernel,
         grid=(steps,),
         out_shape=[*sums.out_shape, jax.ShapeDtypeStruct((TOKENS, D), BF16), TERM, TERM],
-        in_specs=[kept((D, TOKENS)), columns_tile(turn), columns_tile(turn), wide_tile(1, late), wide_tile(1, late), ANY],
+        in_specs=[kept((D, TOKENS)), columns_tile(turn), columns_tile(turn), wide_tile(1, late), wide_tile(1, late), ANY, ANY, ANY],
         out_specs=[VMEM] * 4 + [ANY] * 3,
         scratch_shapes=[
             *STAGES,
             pltpu.VMEM((TOKENS, D), F32),
-            pltpu.VMEM((2, 512, D), BF16),
+            pltpu.VMEM((2, PART, D), BF16),
             PAIR,
+            pltpu.VMEM((2, 2, PART, D), BF16),
+            pltpu.SemaphoreType.DMA((2, 2)),
             *sums.scratch_shapes,
         ],
         compiler_params=pltpu.CompilerParams(collective_id=number, has_side_effects=True, vmem_limit_bytes=VMEM_LIMIT),
         name="second_sums",
-    )(a2t, dg, du, w_gate, w_up, down.reshape(4, 4, 176, D))
-    return d, g, u, squares, da2
+    )(a2t, dg, du, w_gate, w_up, down.reshape(4, 4, 176, D), dy, h1)
+    return d, g, u, squares, dh
 
 
 def first_sums(a1t, dh, gate, up, w_down, down, others, number):
     steps = TILES
     sums = Sums(
         (
-            (DEEP, DOWN, (0,) * 6, FIRST_DOWN),
-            (WIDE, GATE, [2 * n for n in READY], FIRST_WIDE),
-            (WIDE, UP, [2 * n for n in READY], FIRST_WIDE),
+            (DEEP, DOWN, (0,) * 6, lambda begin: FIRST_DOWN),
+            (WIDE, GATE, [2 * n for n in READY], lambda begin: FIRST_WIDE),
+            (WIDE, UP, [2 * n for n in READY], lambda begin: FIRST_WIDE),
         )
     )
 
@@ -756,84 +775,78 @@
         yield last
 
 
+def close_up(padded, closed, rows):
+    def step(t, _):
+        layer, pair = lax.div(t, 16), lax.rem(t, 16)
+        for z in range(4):
+            block = padded[layer, lax.div(pair, 4), lax.rem(pair, 4), pl.ds(48 * z, 48), :]
+            rows[pl.ds(44 * z, 48), :] = block.astype(F32)
+        closed[layer, pair] = rows[pl.ds(0, 176), :].astype(BF16)
+        return 0
+
+    lax.fori_loop(0, 32, step, 0)
+
+
 def gather_kernel(forms, number):
+    shapes = [(2, 4, 4, 4 * WINDOW[f], COLUMNS[f]) for f in forms]
     remote, local = Copies(), Copies()
     jobs = [[GatherJob(form, colour, remote, local) for colour in COLOURS[form]] for form in forms]
 
     def kernel(*refs):
-        owns, outs = refs[: len(forms)], refs[len(forms) : 2 * len(forms)]
-        send, recv, loc = refs[2 * len(forms) :]
+        owns, (*outs, closed) = refs[: len(forms)], refs[len(forms) : 2 * len(forms)]
+        padded, rows, send, recv, loc = refs[2 * len(forms) :]
+        outs.append(padded)
         greet(NEXT)
         order = []
         for m, of_matrix in enumerate(jobs):
             for j, job in enumerate(of_matrix):
                 job.bind(owns[m], outs[m], send, recv, loc)
                 for stage, action in enumerate(job.actions()):
-                    order.append((stage, m, j, action))
+                    order.append((stage if forms[m] == DEEP else stage + 1.5, m, j, action))
+        order.append((6.2, 0, 0, lambda: close_up(padded, closed, rows)))
         for *_, action in sorted(order, key=lambda o: o[:3]):
             action()
 
     def call(*owns):
         return pl.pallas_call(
             kernel,
-            out_shape=[pltpu.VMEM((2, 4, 4, 4 * WINDOW[f], COLUMNS[f]), BF16) for f in forms],
+            out_shape=[pltpu.VMEM(s, BF16) for s in (*shapes[:-1], (2, 16, 176, D))],
             in_specs=[VMEM] * len(forms),
             out_specs=[VMEM] * len(forms),
             scratch_shapes=[
+                pltpu.VMEM(shapes[-1], BF16),
+                pltpu.VMEM((184, D), F32),
                 pltpu.SemaphoreType.DMA((remote.count,)),
                 pltpu.SemaphoreType.DMA((remote.count,)),
                 pltpu.SemaphoreType.DMA((local.count,)),
             ],
-            compiler_params=pltpu.CompilerParams(collective_id=number, has_side_effects=True, vmem_limit_bytes=SMALL_LIMIT),
+            compiler_params=pltpu.CompilerParams(collective_id=number, has_side_effects=True, vmem_limit_bytes=2 * SMALL_LIMIT),
             name="gather",
         )(*(o.reshape(2, 1, 1, WINDOW[f], COLUMNS[f]) for o, f in zip(owns, forms, strict=True)))
 
     return call
 
 
-def settle(gate, up, down):
-    def kernel(gate, up, down, gate_out, up_out, down_out, wide, close, sem, close_sem):
-        copies = [pltpu.make_async_copy(gate, gate_out, sem.at[0]), pltpu.make_async_copy(up, up_out, sem.at[1])]
+def settle(*weights):
+    def kernel(*refs):
+        sem = refs[-1]
+        copies = [
+            pltpu.make_async_copy(refs[n].at[layer], refs[3 + n].at[layer], sem.at[n, layer]) for n in AXES for layer in (0, 1)
+        ]
         for copy in copies:
             copy.start()
-
-        def put(t):
-            return pltpu.make_async_copy(
-                close.at[lax.rem(t, 2)], down_out.at[lax.div(t, 16), lax.rem(t, 16)], close_sem.at[lax.rem(t, 2)]
-            )
-
-        def step(t, _):
-            @pl.when(t >= 2)
-            def _():
-                put(t - 2).wait()
-
-            for z in range(4):
-                block = down[lax.div(t, 16), lax.rem(t, 16), pl.ds(48 * z, 48), :]
-                wide[pl.ds(44 * z, 48), :] = block.astype(F32)
-            close[lax.rem(t, 2)] = wide[pl.ds(0, 176), :].astype(BF16)
-            put(t).start()
-            return 0
-
-        lax.fori_loop(0, 32, step, 0)
-        put(30).wait()
-        put(31).wait()
         for copy in copies:
             copy.wait()
 
     return pl.pallas_call(
         kernel,
-        out_shape=[jax.ShapeDtypeStruct(gate.shape, BF16)] * 2 + [jax.ShapeDtypeStruct((2, 16, 176, D), BF16)],
+        out_shape=[jax.ShapeDtypeStruct(w.shape, BF16) for w in weights],
         in_specs=[VMEM] * 3,
         out_specs=[ANY] * 3,
-        scratch_shapes=[
-            pltpu.VMEM((184, D), F32),
-            pltpu.VMEM((2, 176, D), BF16),
-            PAIR,
-            PAIR,
-        ],
+        scratch_shapes=[pltpu.SemaphoreType.DMA((3, 2))],
         compiler_params=pltpu.CompilerParams(vmem_limit_bytes=SMALL_LIMIT),
         name="settle",
-    )(gate, up, down.reshape(2, 16, 192, D))
+    )(*weights)
 
 
 def through_norm(dy, da, h):
@@ -858,8 +871,8 @@
         z = lax.rem(lax.axis_index("dp"), 4)
         gate1, up1, s1, a1t, h1, a2, a2t = first_layer(x, w_gate, w_up, w_down)
         dg, du, down2 = second_layer(a2, dy, w_gate, w_up, w_down)
-        down_2, gate_2, up_2, squares_2, da2 = second_sums(a2t, dg, du, w_gate, w_up, down2, 0)
-        down1, dh = down_term(s1, dy, da2, h1)
+        down_2, gate_2, up_2, squares_2, dh = second_sums(a2t, dg, du, w_gate, w_up, down2, dy, h1, 0)
+        down1 = down_term(s1, dh)
         down_1, gate_1, up_1, total = first_sums(a1t, dh, gate1, up1, w_down, down1, squares_2, 1)
         gate, up = (gate_1, gate_2), (up_1, up_2)
         down = [lax.dynamic_slice_in_dim(d, 4 * lax.rem(z, 2), 44, 0) for d in (down_1, down_2)]

time: 514 us -> 505 us (0.982)
  Pallas kernels: 504 us -> 494 us
    pallas_call x3, Pallas kernels: 168 us -> 154 us  [the longest x1 125 us: call(): pl.pallas_call(kernel, out_shape=[pltpu.VMEM(s, BF16) for s in (*shapes[:...]
    pallas_call x1, Pallas kernels: 105 us -> 110 us  [second_sums(): pl.pallas_call(kernel, grid=(steps,), out_shape=[*sums.out_shape, jax.Sha...]
where the time goes in v3:
time: 505 us; the launch traced here: 504 us
  Pallas kernels  494 us (98%)
    pallas_call x1, Pallas kernels, call(): pl.pallas_call(kernel, out_shape=[pltpu.VMEM(s, BF16) for s in (*shapes[:...  125 us
    pallas_call x1, Pallas kernels, first_sums(): pl.pallas_call(kernel, grid=(steps,), out_shape=[*sums.out_shape, jax.Sha...  113 us
    pallas_call x1, Pallas kernels, second_sums(): pl.pallas_call(kernel, grid=(steps,), out_shape=[*sums.out_shape, jax.Sha...  110 us
    pallas_call x1, Pallas kernels, second_layer(): pl.pallas_call(kernel, grid=(TILES,), out_shape=[jax.ShapeDtypeStruct((TO...  60.2 us
    pallas_call x1, Pallas kernels, first_layer(): pl.pallas_call(kernel, grid=(TILES,), out_shape=[jax.ShapeDtypeStruct(hid...  56 us
    pallas_call x1, Pallas kernels, down_term(): pl.pallas_call(kernel, grid=(TILES,), out_shape=jax.ShapeDtypeStruct((FF,...  18.2 us
    pallas_call x1, Pallas kernels, settle(): pl.pallas_call(kernel, out_shape=[jax.ShapeDtypeStruct(w.shape, BF16) for...  11.4 us

profile of v3, /device:TPU:0, one launch (start us, length us, event | category | flops | bytes accessed | tf_op | source)
XLA Modules:
  0.0 504.0 jit_solution(7513789013772457703)
XLA Ops:
  0.6 56.0 %first_layer.1 = (f32[2048,2816]{1,0:T(8,128)}, f32[2048,2816]{1,0:T(8,128)}, bf16[2048,2816]{1,0:T(8,128)(2,1)}, bf16[1024,2048]{1,0:T(8,128)(2,1)}, bf16[2048,...) custom-call(bf16[2048,1024]{1,0:T(8,128)(2,1)} %bitcast.28, bf16[2,1024,2816]{2,1,0:T(8,128)(2,1)} %wg.5, ...), custom_call_target="tpu_custom_call" | custom-call | tf_op jit(solution)/shard_map/first_layer/pallas_call | solution.py:408
  56.7 60.2 %second_layer.1 = (bf16[2048,2816]{1,0:T(8,128)(2,1)}, bf16[2048,2816]{1,0:T(8,128)(2,1)}, bf16[2816,1024]{1,0:T(8,128)(2,1)}) custom-call(bf16[2048,1024]{1,0:T(8,128)(2,1)} %get-tuple-element.36.a2, bf16[2048,1024]{1,0:T(8,128)(2,1)} %bitcast.25, bf16[2,1024,2816]{2,1,0:T(8,128)(2,1)} %wg.5, bf16[2,1024,2816]{2,1,0:T(8,128)(2,1)} %wu.5, ...), custom_call_target="tpu_custom_call" | custom-call | tf_op jit(solution)/shard_map/second_layer/pallas_call | solution.py:453
  116.9 110.4 %second_sums.1 = (bf16[48,1024]{1,0:T(8,128)(2,1)}, bf16[16,2816]{1,0:T(8,128)(2,1)}, bf16[16,2816]{1,0:T(8,128)(2,1)}, f32[1,128]{1,0:T(1,128)}, bf16[2048,1024...) custom-call(bf16[1024,2048]{1,0:T(8,128)(2,1)} %get-tuple-element.35.a2t, ...), custom_call_target="tpu_custom_call" | custom-call | tf_op jit(solution)/shard_map/second_sums/pallas_call | solution.py:587
  227.3 18.2 %down_term.1 = bf16[2816,1024]{1,0:T(8,128)(2,1)} custom-call(bf16[2048,2816]{1,0:T(8,128)(2,1)} %get-tuple-element.44.s, bf16[2048,1024]{1,0:T(8,128)(2,1)} %get-tuple-element.41.dh), custom_call_target="tpu_custom_call" | custom-call | tf_op jit(solution)/shard_map/down_term/pallas_call | solution.py:469
  245.5 0.0 copy-start.2
  245.5 0.0 copy-start
  245.5 0.0 copy-start.1
  245.5 0.0 copy-start.3
  245.5 113.0 %first_sums.1 = (bf16[48,1024]{1,0:T(8,128)(2,1)}, bf16[16,2816]{1,0:T(8,128)(2,1)}, bf16[16,2816]{1,0:T(8,128)(2,1)}, f32[1,128]{1,0:T(1,128)}, f32[8,128]{1,0:...) custom-call(bf16[1024,2048]{1,0:T(8,128)(2,1)} %get-tuple-element.34.a1t, ...), custom_call_target="tpu_custom_call" | custom-call | tf_op jit(solution)/shard_map/first_sums/pallas_call | solution.py:652
  358.5 0.0 copy-done.2
  358.6 0.9 dynamic-slice_bitcast_fusion
  359.5 1.2 slice.3
  361.4 0.0 copy-done
  361.4 0.0 copy-done.1
  361.4 1.4 fusion.2
  362.8 0.0 copy-done.3
  362.8 2.9 fusion.13
  365.7 124.8 %gather.1 = (bf16[2,4,4,64,2816]{4,3,2,1,0:T(8,128)(2,1)S(1)}, bf16[2,4,4,64,2816]{4,3,2,1,0:T(8,128)(2,1)S(1)}, bf16[2,16,176,1024]{3,2,1,0:T(8,128)(2,1)S(1)}) custom-call(bf16[2,1,1,16,2816]{4,3,2,1,0:T(8,128)(2,1)S(1)} %get-tuple-element.77.refs_0_, bf16[2,1,1,16,2816]{4,3,2,1,0:T(8,128)(2,1)S(1)} %get-tuple-element.71.refs_1_, ...), custom_call_target="tpu_custom_call" | custom-call | tf_op jit(solution)/shard_map/gather/pallas_call | solution.py:811
  490.6 11.4 %settle.1 = (bf16[2,4,4,64,2816]{4,3,2,1,0:T(8,128)(2,1)}, bf16[2,4,4,64,2816]{4,3,2,1,0:T(8,128)(2,1)}, bf16[2,16,176,1024]{3,2,1,0:T(8,128)(2,1)}) custom-call(bf16[2,4,4,64,2816]{4,3,2,1,0:T(8,128)(2,1)S(1)} %get-tuple-element.53.refs_0_, bf16[2,4,4,64,2816]{4,3,2,1,0:T(8,128)(2,1)S(1)} %get-tuple-element.54.refs_1_, ...), custom_call_target="tpu_custom_call" | custom-call | tf_op jit(solution)/shard_map/settle/pallas_call | solution.py:841
  502.0 1.0 copy.23
  503.0 1.0 copy.24
  (1 shorter events, 0.0 us)
Async XLA Ops:
  245.5 113.0 %copy-start.2 = (bf16[48,1024]{1,0:T(8,128)(2,1)S(1)}, bf16[48,1024]{1,0:T(8,128)(2,1)}, u32[]{:S(2)}) copy-start(bf16[48,1024]{1,0:T(8,128)(2,1)} %get-tuple-element.52) | copy-start | bytes 294916
  245.5 115.9 %copy-start = (f32[2,44,1024]{2,0,1:T(2,128)S(1)}, f32[2,44,1024]{2,0,1:T(2,128)}, u32[]{:S(2)}) copy-start(f32[2,44,1024]{2,0,1:T(2,128)} %param.21) | copy-start | bytes 1081348
  245.5 115.9 %copy-start.1 = (f32[2,44,1024]{2,0,1:T(2,128)S(1)}, f32[2,44,1024]{2,0,1:T(2,128)}, u32[]{:S(2)}) copy-start(f32[2,44,1024]{2,0,1:T(2,128)} %param.18) | copy-start | bytes 1081348
  245.5 117.3 %copy-start.3 = (bf16[16,2816]{1,0:T(8,128)(2,1)S(1)}, bf16[16,2816]{1,0:T(8,128)(2,1)}, u32[]{:S(2)}) copy-start(bf16[16,2816]{1,0:T(8,128)(2,1)} %get-tuple-element.47) | copy-start | bytes 270340

commit v4 on v3

--- a/solution.py
+++ b/solution.py
@@ -36,7 +36,7 @@
     DEEP: laid((384, 384, 256), lambda n: (n,)),
 }
 SECOND_DOWN, SECOND_WIDE, SECOND_LATE = (0, 4, 8, 15, 17, 19, 27), (0, 3, 6, 10, 12, 13, 21), (0, 4, 6, 7, 8, 10, 14)
-FIRST_DOWN, FIRST_WIDE = (0, 5, 9, 19, 21, 42, 70), (0, 3, 8, 13, 28, 50, 69)
+FIRST_DOWN, FIRST_WIDE = (0, 4, 7, 9, 12, 23, 40), (0, 2, 5, 10, 17, 24, 37)
 
 
 def coordinates():
@@ -324,7 +324,7 @@
 
 
 NT, TN = ((1,), (1,)), ((0,), (0,))
-BLOCK, PART = 1024, 256
+BLOCK, PART = 1024, 128
 
 
 def blocks(n, size, body):
@@ -383,7 +383,7 @@
             s[rows, :] = p
             acc[rows, :] += dot(p, wd[...])
 
-        blocks(TOKENS, BLOCK, body)
+        blocks(TOKENS, TOKENS, body)
 
         @pl.when(i == TILES - 1)
         def _():
@@ -462,19 +462,24 @@
     )(a2, dy, w_gate, w_up, w_down)
 
 
-def down_term(s, dh):
-    def kernel(s, dh, out):
+def down_term(s, dh, gate, up, w_down):
+    def kernel(s, dh, gate, up, wd, out, dg, du):
+        def body(rows):
+            ds = dot(dh[rows, :], wd[...], NT).astype(BF16).astype(F32)
+            dg[rows, :], du[rows, :] = through_product(ds, gate[rows, :], up[rows, :])
+
+        blocks(TOKENS, BLOCK, body)
         out[...] = dot(s[...], dh[...], TN).astype(BF16)
 
     return pl.pallas_call(
         kernel,
         grid=(TILES,),
-        out_shape=jax.ShapeDtypeStruct((FF, D), BF16),
-        in_specs=[columns_tile(), kept((TOKENS, D))],
-        out_specs=pl.BlockSpec((TILE, D), lambda i: (i, 0)),
+        out_shape=[jax.ShapeDtypeStruct((FF, D), BF16)] + [jax.ShapeDtypeStruct((TOKENS, FF), BF16)] * 2,
+        in_specs=[columns_tile(), kept((TOKENS, D)), columns_tile(), columns_tile(), deep_tile(0)],
+        out_specs=[pl.BlockSpec((TILE, D), lambda i: (i, 0)), columns_tile(), columns_tile()],
         compiler_params=pltpu.CompilerParams(vmem_limit_bytes=VMEM_LIMIT),
         name="down_term",
-    )(s, dh)
+    )(s, dh, gate, up, w_down)
 
 
 def store_terms(at, dg, du, stage_g, stage_u):
@@ -545,7 +550,7 @@
             def body(rows):
                 acc[rows, :] += dot(dg[rows, :], wg[...], NT) + dot(du[rows, :], wu[...], NT)
 
-            blocks(TOKENS, BLOCK, body)
+            blocks(TOKENS, TOKENS, body)
 
         def take(n):
             rows = pl.ds(PART * n, PART)
@@ -575,7 +580,7 @@
                     da = acc[pl.ds(pl.multiple_of(PART * n + rows.start, 8), rows.size), :].astype(BF16)
                     half[n % 2, rows, :] = through_norm(taken[n % 2, 0, rows, :], da, taken[n % 2, 1, rows, :])
 
-                blocks(PART, PART // 2, body)
+                blocks(PART, PART, body)
                 give(n).start()
             give(parts - 2).wait()
             give(parts - 1).wait()
@@ -605,23 +610,23 @@
     return d, g, u, squares, dh
 
 
-def first_sums(a1t, dh, gate, up, w_down, down, others, number):
+def first_sums(a1t, dg, du, down, others, number):
     steps = TILES
     sums = Sums(
         (
             (DEEP, DOWN, (0,) * 6, lambda begin: FIRST_DOWN),
-            (WIDE, GATE, [2 * n for n in READY], lambda begin: FIRST_WIDE),
-            (WIDE, UP, [2 * n for n in READY], lambda begin: FIRST_WIDE),
+            (WIDE, GATE, READY, lambda begin: FIRST_WIDE),
+            (WIDE, UP, READY, lambda begin: FIRST_WIDE),
         )
     )
 
-    def kernel(a1t, dh, gate, up, wd, down, others, *refs):
+    def kernel(a1t, dg, du, down, others, *refs):
         outs, refs = refs[:4], refs[4:]
-        total, term_g, term_u, stage_g, stage_u, term_sem, dg, du, *refs = refs
+        total, term_g, term_u, stage_g, stage_u, term_sem, *refs = refs
         *refs, got, held, norm_send, norm_recv = refs
         i = pl.program_id(0)
         terms = Terms((stage_g, stage_u), (term_g, term_u), term_sem)
-        enter, reach, rest = sums.run(i, steps, 2, (down, term_g, term_u), outs, refs)
+        enter, reach, rest = sums.run(i, steps, 1, (down, term_g, term_u), outs, refs)
         enter([(axis, by) for axis in AXES for by in AROUND])
 
         @pl.when(i > 0)
@@ -630,12 +635,6 @@
 
         reach(0)
 
-        def body(rows):
-            ds = dot(dh[rows, :], wd[...], NT).astype(BF16).astype(F32)
-            dg[rows, :], du[rows, :] = through_product(ds, gate[rows, :], up[rows, :])
-
-        blocks(TOKENS, BLOCK, body)
-        reach(1)
         store_terms(a1t, dg, du, stage_g, stage_u)
         terms.start(i)
 
@@ -653,12 +652,12 @@
         kernel,
         grid=(steps,),
         out_shape=[*sums.out_shape, jax.ShapeDtypeStruct(SCALAR, F32), TERM, TERM],
-        in_specs=[kept((D, TOKENS)), kept((TOKENS, D)), columns_tile(), columns_tile(), deep_tile(0), ANY, VMEM],
+        in_specs=[kept((D, TOKENS)), columns_tile(), columns_tile(), ANY, VMEM],
         out_specs=[VMEM] * 5 + [ANY] * 2,
-        scratch_shapes=[*STAGES, pltpu.VMEM((TOKENS, TILE), BF16), pltpu.VMEM((TOKENS, TILE), BF16), *sums.scratch_shapes, *NORM],
+        scratch_shapes=[*STAGES, *sums.scratch_shapes, *NORM],
         compiler_params=pltpu.CompilerParams(collective_id=number, has_side_effects=True, vmem_limit_bytes=VMEM_LIMIT),
         name="first_sums",
-    )(a1t, dh, gate, up, w_down, down.reshape(4, 4, 176, D), others)
+    )(a1t, dg, du, down.reshape(4, 4, 176, D), others)
     return d, g, u, total
 
 
@@ -872,8 +871,8 @@
         gate1, up1, s1, a1t, h1, a2, a2t = first_layer(x, w_gate, w_up, w_down)
         dg, du, down2 = second_layer(a2, dy, w_gate, w_up, w_down)
         down_2, gate_2, up_2, squares_2, dh = second_sums(a2t, dg, du, w_gate, w_up, down2, dy, h1, 0)
-        down1 = down_term(s1, dh)
-        down_1, gate_1, up_1, total = first_sums(a1t, dh, gate1, up1, w_down, down1, squares_2, 1)
+        down1, dg, du = down_term(s1, dh, gate1, up1, w_down)
+        down_1, gate_1, up_1, total = first_sums(a1t, dg, du, down1, squares_2, 1)
         gate, up = (gate_1, gate_2), (up_1, up_2)
         down = [lax.dynamic_slice_in_dim(d, 4 * lax.rem(z, 2), 44, 0) for d in (down_1, down_2)]
         gradients = [jnp.stack(g).astype(F32) for g in (gate, up, down)]

time: 505 us -> 510 us (level)
  Pallas kernels: 494 us -> 500 us
    pallas_call x1, Pallas kernels: 18.2 us -> 40.1 us  [down_term(): pl.pallas_call(kernel, grid=(TILES,), out_shape=[jax.ShapeDtypeStruct((FF...]
    pallas_call x1, Pallas kernels: 113 us -> 94.5 us  [first_sums(): pl.pallas_call(kernel, grid=(steps,), out_shape=[*sums.out_shape, jax.Sha...]
where the time goes in v4:
time: 510 us
  Pallas kernels  500 us (98%)
    pallas_call x1, Pallas kernels, call(): pl.pallas_call(kernel, out_shape=[pltpu.VMEM(s, BF16) for s in (*shapes[:...  127 us
    pallas_call x1, Pallas kernels, second_sums(): pl.pallas_call(kernel, grid=(steps,), out_shape=[*sums.out_shape, jax.Sha...  112 us
    pallas_call x1, Pallas kernels, first_sums(): pl.pallas_call(kernel, grid=(steps,), out_shape=[*sums.out_shape, jax.Sha...  94.5 us
    pallas_call x1, Pallas kernels, second_layer(): pl.pallas_call(kernel, grid=(TILES,), out_shape=[jax.ShapeDtypeStruct((TO...  60.2 us
    pallas_call x1, Pallas kernels, first_layer(): pl.pallas_call(kernel, grid=(TILES,), out_shape=[jax.ShapeDtypeStruct(hid...  54.4 us
    pallas_call x1, Pallas kernels, down_term(): pl.pallas_call(kernel, grid=(TILES,), out_shape=[jax.ShapeDtypeStruct((FF...  40.1 us
    pallas_call x1, Pallas kernels, settle(): pl.pallas_call(kernel, out_shape=[jax.ShapeDtypeStruct(w.shape, BF16) for...  11.4 us

profile of v4, /device:TPU:0, one launch (start us, length us, event | category | flops | bytes accessed | tf_op | source)
XLA Modules:
  0.0 509.9 jit_solution(17755398820573662950)
XLA Ops:
  0.6 54.4 %first_layer.1 = (f32[2048,2816]{1,0:T(8,128)}, f32[2048,2816]{1,0:T(8,128)}, bf16[2048,2816]{1,0:T(8,128)(2,1)}, bf16[1024,2048]{1,0:T(8,128)(2,1)}, bf16[2048,...) custom-call(bf16[2048,1024]{1,0:T(8,128)(2,1)} %bitcast.28, bf16[2,1024,2816]{2,1,0:T(8,128)(2,1)} %wg.5, ...), custom_call_target="tpu_custom_call" | custom-call | tf_op jit(solution)/shard_map/first_layer/pallas_call | solution.py:408
  55.0 60.2 %second_layer.1 = (bf16[2048,2816]{1,0:T(8,128)(2,1)}, bf16[2048,2816]{1,0:T(8,128)(2,1)}, bf16[2816,1024]{1,0:T(8,128)(2,1)}) custom-call(bf16[2048,1024]{1,0:T(8,128)(2,1)} %get-tuple-element.40.a2, bf16[2048,1024]{1,0:T(8,128)(2,1)} %bitcast.24, bf16[2,1024,2816]{2,1,0:T(8,128)(2,1)} %wg.5, bf16[2,1024,2816]{2,1,0:T(8,128)(2,1)} %wu.5, ...), custom_call_target="tpu_custom_call" | custom-call | tf_op jit(solution)/shard_map/second_layer/pallas_call | solution.py:453
  115.3 112.1 %second_sums.1 = (bf16[48,1024]{1,0:T(8,128)(2,1)}, bf16[16,2816]{1,0:T(8,128)(2,1)}, bf16[16,2816]{1,0:T(8,128)(2,1)}, f32[1,128]{1,0:T(1,128)}, bf16[2048,1024...) custom-call(bf16[1024,2048]{1,0:T(8,128)(2,1)} %get-tuple-element.39.a2t, ...), custom_call_target="tpu_custom_call" | custom-call | tf_op jit(solution)/shard_map/second_sums/pallas_call | solution.py:592
  227.4 40.1 %down_term.1 = (bf16[2816,1024]{1,0:T(8,128)(2,1)}, bf16[2048,2816]{1,0:T(8,128)(2,1)}, bf16[2048,2816]{1,0:T(8,128)(2,1)}) custom-call(bf16[2048,2816]{1,0:T(8,128)(2,1)} %get-tuple-element.38.s, bf16[2048,1024]{1,0:T(8,128)(2,1)} %get-tuple-element.45.dh, f32[2048,2816]{1,0:T(8,128)} %get-tuple-element.46.gate, f32[2048,2816]{1,0:T(8,128)} %get-tuple-element.47.up, ...), custom_call_target="tpu_custom_call" | custom-call | tf_op jit(solution)/shard_map/down_term/pallas_call | solution.py:474
  267.4 0.0 copy-start.2
  267.5 0.0 copy-start
  267.5 0.0 copy-start.1
  267.5 0.0 copy-start.3
  267.5 94.5 %first_sums.1 = (bf16[48,1024]{1,0:T(8,128)(2,1)}, bf16[16,2816]{1,0:T(8,128)(2,1)}, bf16[16,2816]{1,0:T(8,128)(2,1)}, f32[1,128]{1,0:T(1,128)}, f32[8,128]{1,0:...) custom-call(bf16[1024,2048]{1,0:T(8,128)(2,1)} %get-tuple-element.37.a1t, ...), custom_call_target="tpu_custom_call" | custom-call | tf_op jit(solution)/shard_map/first_sums/pallas_call | solution.py:651
  362.0 0.0 copy-done.2
  362.0 0.9 dynamic-slice_bitcast_fusion
  363.0 1.2 slice.3
  364.9 0.0 copy-done
  364.9 0.0 copy-done.1
  364.9 1.4 fusion.2
  366.3 0.0 copy-done.3
  366.3 2.9 fusion.13
  369.2 127.2 %gather.1 = (bf16[2,4,4,64,2816]{4,3,2,1,0:T(8,128)(2,1)S(1)}, bf16[2,4,4,64,2816]{4,3,2,1,0:T(8,128)(2,1)S(1)}, bf16[2,16,176,1024]{3,2,1,0:T(8,128)(2,1)S(1)}) custom-call(bf16[2,1,1,16,2816]{4,3,2,1,0:T(8,128)(2,1)S(1)} %get-tuple-element.83.refs_0_, bf16[2,1,1,16,2816]{4,3,2,1,0:T(8,128)(2,1)S(1)} %get-tuple-element.77.refs_1_, ...), custom_call_target="tpu_custom_call" | custom-call | tf_op jit(solution)/shard_map/gather/pallas_call | solution.py:810
  496.4 11.4 %settle.1 = (bf16[2,4,4,64,2816]{4,3,2,1,0:T(8,128)(2,1)}, bf16[2,4,4,64,2816]{4,3,2,1,0:T(8,128)(2,1)}, bf16[2,16,176,1024]{3,2,1,0:T(8,128)(2,1)}) custom-call(bf16[2,4,4,64,2816]{4,3,2,1,0:T(8,128)(2,1)S(1)} %get-tuple-element.59.refs_0_, bf16[2,4,4,64,2816]{4,3,2,1,0:T(8,128)(2,1)S(1)} %get-tuple-element.60.refs_1_, ...), custom_call_target="tpu_custom_call" | custom-call | tf_op jit(solution)/shard_map/settle/pallas_call | solution.py:840
  507.9 1.0 copy.23
  508.9 1.0 copy.24
  (1 shorter events, 0.0 us)
Async XLA Ops:
  267.4 94.6 %copy-start.2 = (bf16[48,1024]{1,0:T(8,128)(2,1)S(1)}, bf16[48,1024]{1,0:T(8,128)(2,1)}, u32[]{:S(2)}) copy-start(bf16[48,1024]{1,0:T(8,128)(2,1)} %get-tuple-element.58) | copy-start | bytes 294916
  267.5 97.4 %copy-start = (f32[2,44,1024]{2,0,1:T(2,128)S(1)}, f32[2,44,1024]{2,0,1:T(2,128)}, u32[]{:S(2)}) copy-start(f32[2,44,1024]{2,0,1:T(2,128)} %param.21) | copy-start | bytes 1081348
  267.5 97.4 %copy-start.1 = (f32[2,44,1024]{2,0,1:T(2,128)S(1)}, f32[2,44,1024]{2,0,1:T(2,128)}, u32[]{:S(2)}) copy-start(f32[2,44,1024]{2,0,1:T(2,128)} %param.18) | copy-start | bytes 1081348
  267.5 98.8 %copy-start.3 = (bf16[16,2816]{1,0:T(8,128)(2,1)S(1)}, bf16[16,2816]{1,0:T(8,128)(2,1)}, u32[]{:S(2)}) copy-start(bf16[16,2816]{1,0:T(8,128)(2,1)} %get-tuple-element.53) | copy-start | bytes 270340
